TPU v7x, 256 devices: a 8x8x2 block of a 8x8x16 slice. The times are simulated.
256 devices in a mesh: groups: 2 (over z), dev: 16 (over y, core), tp: 8 (over x).
Axes of the slice: x: 8, y: 8, z: 2, core: 2. Of those that a mesh axis runs over, the one named last changes fastest.
The devices are a block of a 8x8x16 slice.
Arguments:
- hidden_states: bfloat16 [20480, 5120], P(('groups', 'dev'), 'tp'), parts along dimension 0, may hold values from -6 to 6
- norm_gain: bfloat16 [5120], replicated, may hold values from 0.25 to 1.75
- w_query: bfloat16 [5120, 5120], P('dev', 'tp'), may hold values from -2 to 2
- w_key: bfloat16 [5120, 1024], P('dev', 'tp'), may hold values from -2 to 2
- w_value: bfloat16 [5120, 1024], P('dev', 'tp'), may hold values from -0.078125 to 0.078125
- prompt_blocks: int32 [16], P('groups'), parts along dimension 0, may hold values from 1 to 11, 80 in all
- owner_map: int32 [160], P(('groups', 'dev')), parts along dimension 0, may hold values from 0 to 15, as said below
- slot_table: int32 [32, 32], P(('groups', 'dev')), parts along dimension 0, may hold values from 0 to 31, each once within a row
Outputs:
- context: bfloat16 [20480, 5120], P(('groups', 'dev'), 'tp'), parts along dimension 0
- kv_cache: bfloat16 [1024, 128, 2048], P(('groups', 'dev'), None, 'tp'), parts along dimension 0
There are 2 independent parts, one for each index of `groups`. A program takes and returns all parts, laid end to end along the dimension named above; an argument that names none is the same for every part. Nothing has to cross between parts.
Inputs may be any that keep to these rules, and one draw needn't show every extreme that they name: `prompt_blocks`: the entries sum to 80. `owner_map`: each device's 5 blocks name any owner at most 2 times, and no owner receives more than 32 blocks; in every draw some owner receives 2 blocks from every device. `slot_table`: each row is a permutation of 0 to 31.
All inputs are finite; a program needn't handle non-finite values.
Results may differ from a plain program's by a relative error of at most 0.0079.
Values may be sent and summed in bfloat16 or wider, within the bound.
No kernel may reach another device: no remote copies, remote signals or barrier semaphores. Data moves between devices by JAX's collectives and lax.ppermute only.
A program may use at most 128 MiB of HBM per device.

v0:
```python
import functools
import math

import jax
import jax.numpy as jnp
from jax import lax
from jax.experimental import pallas as pl
from jax.experimental.pallas import tpu as pltpu
from jax.sharding import PartitionSpec as P


HD = 128
BLOCK = 128
LEN_BLOCKS = 11
EPSILON = 1e-06
THETA = 1000000.0
HBM = pltpu.MemorySpace.HBM
VMEM = pltpu.MemorySpace.VMEM
SMEM = pltpu.MemorySpace.SMEM
MIB = 1024 * 1024


def ring(block, axis, hop, last_ahead, tied=None):
    size = lax.axis_size(axis)
    count = size // hop
    ahead = [(i, (i + hop) % size) for i in range(size)]
    back = [(i, (i - hop) % size) for i in range(size)]
    got = {0: block}
    up = down = block
    for step in range(1, count // 2):
        up = lax.ppermute(up, axis, ahead)
        down = lax.ppermute(down, axis, back)
        got[count - step] = up
        got[step] = down
        if tied and step == 1:
            up, *tied[:] = lax.optimization_barrier((up, *tied))
    if last_ahead:
        got[count // 2] = lax.ppermute(up, axis, ahead)
    else:
        got[count // 2] = lax.ppermute(down, axis, back)
    return [got[i] for i in range(count)]


def swap(block, axis):
    size = lax.axis_size(axis)
    return lax.ppermute(block, axis, [(i, i ^ 1) for i in range(size)])


def by_arrival(count):
    order = [0]
    for step in range(1, count // 2):
        order += [step, count - step]
    return order


def weight_copies(place, weights, wbuf, sem, count, feat, lo, width):
    tp, chip, core = place[0], place[1], place[2]
    mine, other, mine_mid, other_mid = weights
    w_rows = feat // 2
    copies = []
    for k, rel in enumerate([*by_arrival(count), count // 2]):
        i = jnp.bitwise_and(chip + rel - tp, count - 1)
        for which in range(2):
            spot = core if which == 0 else 1 - core
            if rel == count // 2:
                src = mine_mid if which == 0 else other_mid
            else:
                src = (mine if which == 0 else other).at[k]
            copies.append(
                pltpu.make_async_copy(
                    src.at[pl.ds(0, w_rows), pl.ds(lo, width)],
                    wbuf.at[pl.ds(pl.multiple_of(i * feat + spot * w_rows, 64), w_rows)],
                    sem.at[2 * rel + which],
                )
            )
    return copies


def rotated(head, cos, sin):
    return (head * cos[...] + pltpu.roll(head, HD // 2, 1) * sin[...]).astype(jnp.bfloat16)


def normalize(pieces, gain, out):
    rows, feat = pieces[0].shape
    tile = 32

    def one_tile(r, unused):
        at_rows = pl.ds(pl.multiple_of(r * tile, tile), tile)
        totals = [jnp.zeros((tile, 128), jnp.float32) for _ in range(2)]
        for piece in pieces:
            for g in range(feat // 128):
                part = piece[at_rows, g * 128 : (g + 1) * 128].astype(jnp.float32)
                totals[g % 2] = totals[g % 2] + part * part
        mean = jnp.sum(totals[0] + totals[1], axis=1, keepdims=True) * (1.0 / (feat * len(pieces)))
        scale = jnp.broadcast_to(lax.rsqrt(mean + EPSILON), (tile, 128))
        for i, piece in enumerate(pieces):
            for g in range(feat // 128):
                part = piece[at_rows, g * 128 : (g + 1) * 128].astype(jnp.float32)
                at_col = slice(i * feat + g * 128, i * feat + (g + 1) * 128)
                out[at_rows, at_col] = (part * scale * gain[:, at_col]).astype(jnp.bfloat16)
        return unused

    lax.fori_loop(0, rows // tile, one_tile, 0)


def norm_kernel(*refs):
    normalize(refs[:-2], refs[-2], refs[-1])


def norm_rows(pieces, gain):
    count = len(pieces)
    rows, feat = pieces[0].shape
    return pl.pallas_call(
        norm_kernel,
        out_shape=jax.ShapeDtypeStruct((rows, count * feat), jnp.bfloat16),
        in_specs=[pl.BlockSpec(memory_space=VMEM)] * (count + 1),
        out_specs=pl.BlockSpec(memory_space=VMEM),
        compiler_params=pltpu.CompilerParams(vmem_limit_bytes=12 * MIB),
        cost_estimate=pl.CostEstimate(
            flops=6 * rows * feat * count, bytes_accessed=4 * rows * feat * count, transcendentals=0
        ),
    )(*pieces, gain)


def keys_kernel(place, x_a, *refs, count, feat, lo):
    pieces = refs[:count]
    weights = refs[count : count + 4]
    gain, cos, sin, kv, labels, x_b = refs[count + 4 : count + 10]
    wbuf, acc, tags, sem_w, sem_tag = refs[count + 10 :]
    w_rows = feat // 2
    mid = count // 2
    part = x_a.shape[0]
    w_copies = weight_copies(place, weights, wbuf, sem_w, count, feat, lo, 2 * HD)
    t_copies = []
    for which in range(2):
        for k, rel in enumerate([*by_arrival(count), mid]):
            src = weights[2 + which] if rel == mid else weights[which].at[k]
            t_copies.append(
                pltpu.make_async_copy(
                    src.at[pl.ds(w_rows, 8), pl.ds(0, 128)],
                    tags.at[which * count + rel],
                    sem_tag.at[which * count + rel],
                )
            )
    for copy in w_copies + t_copies:
        copy.start()
    normalize(pieces, gain, x_b)
    for copy in w_copies + t_copies:
        copy.wait()
    acc[:part] = jnp.dot(x_a[...], wbuf[...], preferred_element_type=jnp.float32)
    acc[part:] = jnp.dot(x_b[...], wbuf[...], preferred_element_type=jnp.float32)
    kv[:, :HD] = rotated(acc[:, :HD], cos, sin)
    kv[:, HD:] = acc[:, HD:].astype(jnp.bfloat16)
    for r in range(2 * count):
        labels[r : r + 1, :] = tags[r].astype(jnp.float32)[0:1].astype(jnp.int32)


def queries_kernel(place, x_a, x_b, mine, other, mine_mid, other_mid, cos, sin, q, wbuf, acc, sem_w, *, count, feat, heads):
    part = x_a.shape[0]
    weights = (mine, other, mine_mid, other_mid)
    w_copies = weight_copies(place, weights, wbuf, sem_w, count, feat, 0, heads * HD)
    for copy in w_copies:
        copy.start()
    for copy in w_copies:
        copy.wait()
    for half, x in enumerate((x_a, x_b)):
        rows = pl.ds(half * part, part)
        acc[...] = jnp.dot(x[...], wbuf[...], preferred_element_type=jnp.float32)
        for h in range(heads):
            q[h, rows] = rotated(acc[:, h * HD : (h + 1) * HD], cos.at[rows], sin.at[rows])


def project_keys(place, x_a, pieces, weights, gain, cos, sin, lo):
    count = len(pieces)
    part, feat = pieces[0].shape
    tok = 2 * part
    return pl.pallas_call(
        functools.partial(keys_kernel, count=count, feat=feat, lo=lo),
        out_shape=(
            jax.ShapeDtypeStruct((tok, 2 * HD), jnp.bfloat16),
            jax.ShapeDtypeStruct((2 * count, 128), jnp.int32),
            jax.ShapeDtypeStruct((part, count * feat), jnp.bfloat16),
        ),
        in_specs=[pl.BlockSpec(memory_space=SMEM)]
        + [pl.BlockSpec(memory_space=VMEM)] * (count + 1)
        + [pl.BlockSpec(memory_space=HBM)]
        + [pl.BlockSpec(memory_space=pl.ANY)] * 3
        + [pl.BlockSpec(memory_space=VMEM)] * 3,
        out_specs=(pl.BlockSpec(memory_space=VMEM),) * 3,
        scratch_shapes=[
            pltpu.VMEM((count * feat, 2 * HD), jnp.bfloat16),
            pltpu.VMEM((tok, 2 * HD), jnp.float32),
            pltpu.VMEM((2 * count, 8, 128), jnp.bfloat16),
            pltpu.SemaphoreType.DMA((2 * count,)),
            pltpu.SemaphoreType.DMA((2 * count,)),
        ],
        compiler_params=pltpu.CompilerParams(vmem_limit_bytes=20 * MIB),
        cost_estimate=pl.CostEstimate(
            flops=4 * tok * feat * count * HD, bytes_accessed=4 * tok * feat * count, transcendentals=0
        ),
    )(place, x_a, *pieces, *weights, gain, cos, sin)


def project_queries(place, x_a, x_b, weights, cos, sin, heads):
    count = weights[0].shape[0] + 1
    part = x_a.shape[0]
    tok = 2 * part
    feat = x_a.shape[1] // count
    width = heads * HD
    return pl.pallas_call(
        functools.partial(queries_kernel, count=count, feat=feat, heads=heads),
        out_shape=jax.ShapeDtypeStruct((heads, tok, HD), jnp.bfloat16),
        in_specs=[pl.BlockSpec(memory_space=SMEM)]
        + [pl.BlockSpec(memory_space=VMEM)] * 2
        + [pl.BlockSpec(memory_space=HBM)]
        + [pl.BlockSpec(memory_space=pl.ANY)] * 3
        + [pl.BlockSpec(memory_space=VMEM)] * 2,
        out_specs=pl.BlockSpec(memory_space=VMEM),
        scratch_shapes=[
            pltpu.VMEM((count * feat, width), jnp.bfloat16),
            pltpu.VMEM((part, width), jnp.float32),
            pltpu.SemaphoreType.DMA((2 * count,)),
        ],
        compiler_params=pltpu.CompilerParams(vmem_limit_bytes=20 * MIB),
        cost_estimate=pl.CostEstimate(
            flops=2 * tok * feat * count * width, bytes_accessed=2 * tok * feat * count, transcendentals=0
        ),
    )(place, x_a, x_b, *weights, cos, sin)


def attend_kernel(
    info, q_in, far, near, own, *refs, lo, hi
):
    out, qbuf, kvbuf, sbuf, mbuf, lbuf, obuf, tbuf, sems, sem_out = refs[-10:]
    heads = q_in.shape[0]
    tok = own.shape[0]
    local = tok // BLOCK
    back = 2 * local
    span_in = pl.ds(lo * BLOCK, (hi - lo) * BLOCK)
    copies = [
        pltpu.make_async_copy(q_in.at[:, span_in], qbuf.at[:, span_in], sems.at[0]),
        pltpu.make_async_copy(far, kvbuf.at[pl.ds(BLOCK, tok)], sems.at[1]),
        pltpu.make_async_copy(near, kvbuf.at[pl.ds(BLOCK + tok, tok)], sems.at[2]),
        pltpu.make_async_copy(own, kvbuf.at[pl.ds(BLOCK + 2 * tok, tok)], sems.at[3]),
    ]
    for copy in copies:
        copy.start()
    kvbuf[:BLOCK] = jnp.zeros((BLOCK, 2 * HD), jnp.bfloat16)
    for copy in copies:
        copy.wait()
    first = info[0]
    n_prompts = info.shape[0] - 1
    factor = math.log2(math.e) / math.sqrt(HD)
    rows = heads * BLOCK
    row = lax.broadcasted_iota(jnp.int32, (BLOCK, BLOCK), 0)
    col = lax.broadcasted_iota(jnp.int32, (BLOCK, BLOCK), 1)
    causal = col <= row

    def result_copy(i):
        at = pl.ds(pl.multiple_of(i * BLOCK, BLOCK), BLOCK)
        return pltpu.make_async_copy(tbuf.at[i - lo], out.at[at], sem_out.at[i - lo])

    def one_block(i, unused):
        block = first + i

        def find(p, state):
            start, best = state
            best = jnp.where(start <= block, start, best)
            return start + info[1 + p], best

        _, begin = lax.fori_loop(0, n_prompts, find, (jnp.int32(0), jnp.int32(0)))
        low = jnp.maximum(begin - first + back, i) + 1
        last = back + i + 1
        pairs = (last - low + 2) // 2
        q = qbuf[:, pl.ds(pl.multiple_of(i * BLOCK, BLOCK), BLOCK), :].reshape(rows, HD)

        def span(t):
            return pl.ds(pl.multiple_of((last - 1 - 2 * t) * BLOCK, BLOCK), 2 * BLOCK)

        def score(t, h):
            s = lax.dot_general(
                q[h * BLOCK : (h + 1) * BLOCK],
                kvbuf[span(t), :HD],
                (((1,), (1,)), ((), ())),
                preferred_element_type=jnp.float32,
            )
            inside = last - 1 - 2 * t >= low
            bias = jnp.where(inside, 0.0, -1e30)
            return s[:, :BLOCK] * factor + bias, s[:, BLOCK:] * factor

        mbuf[...] = jnp.full_like(mbuf, -1e30)

        def upward(t, unused):
            shut = jnp.where(t == 0, -1e30, 0.0)
            for h in range(heads):
                at = slice(h * BLOCK, (h + 1) * BLOCK)
                left, right = score(t, h)
                right = right + jnp.where(causal, 0.0, shut)
                sbuf[t, at, :BLOCK] = left
                sbuf[t, at, BLOCK:] = right
                mbuf[at] = jnp.maximum(mbuf[at], jnp.maximum(left, right))
            return unused

        lax.fori_loop(0, pairs, upward, 0)
        top = jnp.max(mbuf[...], axis=1, keepdims=True)
        mbuf[...] = jnp.broadcast_to(top, mbuf.shape)
        lbuf[...] = jnp.zeros_like(lbuf)
        obuf[...] = jnp.zeros_like(obuf)

        def gather(t, unused):
            for h in range(heads):
                at = slice(h * BLOCK, (h + 1) * BLOCK)
                peak = mbuf[at]
                left = jnp.exp2(sbuf[t, at, :BLOCK] - peak)
                right = jnp.exp2(sbuf[t, at, BLOCK:] - peak)
                lbuf[at] += left + right
                p = jnp.concatenate([left.astype(jnp.bfloat16), right.astype(jnp.bfloat16)], axis=1)
                obuf[at] += jnp.dot(p, kvbuf[span(t), HD:], preferred_element_type=jnp.float32)
            return unused

        lax.fori_loop(0, pairs, gather, 0)
        total = jnp.sum(lbuf[...], axis=1, keepdims=True)
        result = (obuf[...] / total).astype(jnp.bfloat16)
        for h in range(heads):
            tbuf[i - lo, :, h * HD : (h + 1) * HD] = result[h * BLOCK : (h + 1) * BLOCK]
        result_copy(i).start()
        return unused

    lax.fori_loop(lo, hi, one_block, 0)
    for i in range(lo, hi):
        result_copy(i).wait()


def attend(info, q, far, near, own, lo, hi, base=None):
    heads = q.shape[0]
    tok = own.shape[0]
    operands = [info, q, far, near, own]
    if base is not None:
        operands.append(base)
    return pl.pallas_call(
        functools.partial(attend_kernel, lo=lo, hi=hi),
        out_shape=jax.ShapeDtypeStruct((tok, heads * HD), jnp.bfloat16),
        in_specs=[pl.BlockSpec(memory_space=SMEM)]
        + [pl.BlockSpec(memory_space=pl.ANY)] * (len(operands) - 1),
        out_specs=pl.BlockSpec(memory_space=pl.ANY),
        scratch_shapes=[
            pltpu.VMEM((heads, tok, HD), jnp.bfloat16),
            pltpu.VMEM((3 * tok + BLOCK, 2 * HD), jnp.bfloat16),
            pltpu.VMEM(((LEN_BLOCKS + 1) // 2, heads * BLOCK, 2 * BLOCK), jnp.float32),
            pltpu.VMEM((heads * BLOCK, BLOCK), jnp.float32),
            pltpu.VMEM((heads * BLOCK, BLOCK), jnp.float32),
            pltpu.VMEM((heads * BLOCK, HD), jnp.float32),
            pltpu.VMEM((hi - lo, BLOCK, heads * HD), jnp.bfloat16),
            pltpu.SemaphoreType.DMA((4,)),
            pltpu.SemaphoreType.DMA((hi - lo,)),
        ],
        input_output_aliases={5: 0} if base is not None else {},
        compiler_params=pltpu.CompilerParams(vmem_limit_bytes=12 * MIB),
        cost_estimate=pl.CostEstimate(
            flops=2 * 10**9 * (hi - lo), bytes_accessed=4 * 10**6, transcendentals=10**6
        ),
    )(*operands)


def cache_kernel(place, labels, table, mine, other, mine_mid, other_mid, out, sem, *, local, count, tok):
    chip, core, me = place[1], place[2], place[3]
    mid = count // 2
    slots = out.shape[0]

    def put(src, at_row, slot):
        return pltpu.make_async_copy(src.at[pl.ds(pl.multiple_of(at_row, BLOCK), BLOCK)], out.at[slot], sem)

    def one(source, rank):
        rel = jnp.bitwise_and(jnp.right_shift(source, 1) - chip, count - 1)
        same = jnp.bitwise_and(source, 1) == core
        middle = rel == mid
        spot = jnp.where(rel > mid, 2 * (count - rel), jnp.where(middle, 0, jnp.maximum(2 * rel - 1, 0)))
        label_row = jnp.where(same, rel, count + rel)
        for inner in range(local):
            hit = labels[label_row, inner] == me

            @pl.when(hit)
            def _():
                slot = table[0, rank]
                at_row = spot * tok + inner * BLOCK

                @pl.when(same & jnp.logical_not(middle))
                def _():
                    put(mine, at_row, slot).start()

                @pl.when(jnp.logical_not(same) & jnp.logical_not(middle))
                def _():
                    put(other, at_row, slot).start()

                @pl.when(same & middle)
                def _():
                    put(mine_mid, at_row, slot).start()

                @pl.when(jnp.logical_not(same) & middle)
                def _():
                    put(other_mid, at_row, slot).start()

            rank = rank + hit.astype(jnp.int32)
        return rank

    found = lax.fori_loop(0, 2 * count, one, jnp.int32(0))

    def clear(r, unused):
        out[table[0, r]] = jnp.zeros(out.shape[1:], out.dtype)
        return unused

    lax.fori_loop(found, slots, clear, 0)

    def settle(r, unused):
        put(mine, 0, 0).wait()
        return unused

    lax.fori_loop(0, found, settle, 0)


def fill_cache(place, labels, table, mine, other, mine_mid, other_mid, local, count):
    tok = mine_mid.shape[0]
    slots = table.shape[1]
    return pl.pallas_call(
        functools.partial(cache_kernel, local=local, count=count, tok=tok),
        out_shape=jax.ShapeDtypeStruct((slots, BLOCK, mine.shape[1]), jnp.bfloat16),
        in_specs=[pl.BlockSpec(memory_space=SMEM)] * 3 + [pl.BlockSpec(memory_space=pl.ANY)] * 4,
        out_specs=pl.BlockSpec(memory_space=VMEM),
        scratch_shapes=[pltpu.SemaphoreType.DMA],
        compiler_params=pltpu.CompilerParams(vmem_limit_bytes=8 * MIB),
    )(place, labels, table, mine, other, mine_mid, other_mid)


def on_device(
    hidden_states, norm_gain, w_query, w_key, w_value, prompt_blocks, owner_map, slot_table
):
    tok, feat = hidden_states.shape
    n_dev = lax.axis_size("dev")
    n_tp = lax.axis_size("tp")
    device = lax.axis_index("dev")
    count = n_dev // 2
    assert count & (count - 1) == 0 and count == n_tp
    mid = count // 2
    local = tok // BLOCK
    heads = w_query.shape[1] // HD
    place = jnp.stack([lax.axis_index("tp"), device // 2, device % 2, device]).astype(jnp.int32)

    token_rows = device * tok + jnp.arange(tok, dtype=jnp.int32)
    starts = (jnp.cumsum(prompt_blocks) - prompt_blocks) * BLOCK
    start_of = jnp.max(jnp.where(token_rows[:, None] >= starts[None, :], starts[None, :], 0), axis=1)
    offsets = token_rows - start_of
    lane = jnp.arange(HD, dtype=jnp.int32)
    freq_index = lax.rem(lane, HD // 2).astype(jnp.float32)
    inverse = jnp.exp(freq_index * (-2.0 * math.log(THETA) / HD))
    angles = offsets.astype(jnp.float32)[:, None] * inverse[None, :]
    cos = jnp.cos(angles)
    sin = jnp.sin(angles) * jnp.where(lane < HD // 2, -1.0, 1.0)[None, :]
    gain = norm_gain.astype(jnp.float32)
    gain = lax.dynamic_slice_in_dim(
        jnp.concatenate([gain, gain]), lax.axis_index("tp") * feat, n_tp * feat
    )[None]
    info = jnp.concatenate([(device * local)[None].astype(jnp.int32), prompt_blocks])

    part = tok // 2
    tied = [cos, sin, gain, place, info]
    x_a = ring(hidden_states[:part], "tp", 1, True)
    x_b = ring(hidden_states[part:], "tp", 1, False, tied)
    cos, sin, gain, place, info = tied

    weights = jnp.concatenate([w_query, w_key, w_value], axis=1)
    w_cols = weights.shape[1]
    labels = jnp.pad(owner_map.astype(jnp.bfloat16)[None], ((0, 7), (0, w_cols - local)))
    weights = jnp.concatenate([weights, labels], axis=0)
    arrival = by_arrival(count)
    w_got = ring(weights, "dev", 2, True)
    w_mine = jnp.stack([w_got[i] for i in arrival])
    w_other = swap(w_mine, "dev")
    w_other_mid = swap(w_got[mid], "dev")
    w_set = (w_mine, w_other, w_got[mid], w_other_mid)

    n_a = norm_rows(x_a, gain)
    kv, labels, n_b = project_keys(place, n_a, x_b, w_set, gain, cos, sin, heads * HD)
    q = project_queries(place, n_a, n_b, w_set, cos, sin, heads)

    near = lax.ppermute(kv, "dev", [(i, i + 1) for i in range(n_dev - 1)])
    k_got = ring(kv, "dev", 2, False)
    far = k_got[count - 1]
    cuts = (0, local // 2, local - 1, local)
    context = attend(info, q, far, near, kv, cuts[0], cuts[1])
    context = attend(info, q, far, near, kv, cuts[1], cuts[2], base=context)
    context = attend(info, q, far, near, kv, cuts[2], cuts[3], base=context)
    k_mine = jnp.concatenate([k_got[i] for i in arrival], axis=0)
    k_other = swap(k_mine, "dev")
    k_mid_other = swap(k_got[mid], "dev")
    kv_cache = fill_cache(
        place, labels, slot_table, k_mine, k_other, k_got[mid], k_mid_other, local, count
    )
    return (context, kv_cache)


def solution(mesh):
    in_specs = (
        P(("groups", "dev"), "tp"),
        P(),
        P("dev", "tp"),
        P("dev", "tp"),
        P("dev", "tp"),
        P("groups"),
        P(("groups", "dev")),
        P(("groups", "dev"), None),
    )
    out_specs = (P(("groups", "dev"), "tp"), P(("groups", "dev"), None, "tp"))

    return jax.shard_map(on_device, mesh=mesh, in_specs=in_specs, out_specs=out_specs, check_vma=False)
```

profile of v0, /device:TPU:513, one launch (start us, length us, event | category | flops | bytes accessed | tf_op | source)
XLA Modules:
  0.0 201.5 jit_solution(12004561075207974465)
XLA Ops:
  1.3 1.1 fusion.1
  2.4 12.5 %collective-permute-start.14 = (bf16[328,896]{1,0:T(8,128)(2,1)S(1)}, bf16[328,896]{1,0:T(8,128)(2,1)S(1)}, u32[]{:S(2)}, u32[]{:S(2)}) collective-permute-start(bf16[328,896]{1,0:T(8,128)(2,1)S(1)} %fusion.1), channel_id=1, source_target_pairs={{0,112},{8,120},{16,0},{24,8},{32,16},{40,24},{48,32},{56,40},{64,... | collective-permute-start | bytes 1763336 | tf_op jit(solution)/shard_map/ppermute | solution.py:32
  15.0 6.8 %collective-permute-done.14 = bf16[328,896]{1,0:T(8,128)(2,1)S(1)} collective-permute-done((bf16[328,896]{1,0:T(8,128)(2,1)S(1)}, bf16[328,896]{1,0:T(8,128)(2,1)S(1)}, u32[]{:S(2)}, u32[]{:S(2)}) %collective-permute-start.14) | collective-permute-done | bytes 587808 | tf_op jit(solution)/shard_map/ppermute | solution.py:32
  21.8 5.4 %collective-permute-start.16 = (bf16[328,896]{1,0:T(8,128)(2,1)S(1)}, bf16[328,896]{1,0:T(8,128)(2,1)S(1)}, u32[]{:S(2)}, u32[]{:S(2)}) collective-permute-start(bf16[328,896]{1,0:T(8,128)(2,1)S(1)} %collective-permute-done.14), channel_id=1, source_target_pairs={{0,112},{8,120},{16,0},{24,8},{32,16},{40,24},{48,32},{56,40},{64,... | collective-permute-start | bytes 1763336 | tf_op jit(solution)/shard_map/ppermute | solution.py:32
  27.2 2.0 bitcast_dynamic-update-slice_fusion.6
  29.1 0.9 bitcast_dynamic-update-slice_fusion.5
  30.0 6.3 %collective-permute-done.16 = bf16[328,896]{1,0:T(8,128)(2,1)S(1)} collective-permute-done((bf16[328,896]{1,0:T(8,128)(2,1)S(1)}, bf16[328,896]{1,0:T(8,128)(2,1)S(1)}, u32[]{:S(2)}, u32[]{:S(2)}) %collective-permute-start.16) | collective-permute-done | bytes 587808 | tf_op jit(solution)/shard_map/ppermute | solution.py:32
  36.3 3.1 %collective-permute-start.18 = (bf16[328,896]{1,0:T(8,128)(2,1)S(1)}, bf16[328,896]{1,0:T(8,128)(2,1)S(1)}, u32[]{:S(2)}, u32[]{:S(2)}) collective-permute-start(bf16[328,896]{1,0:T(8,128)(2,1)S(1)} %collective-permute-done.16), channel_id=1, source_target_pairs={{0,112},{8,120},{16,0},{24,8},{32,16},{40,24},{48,32},{56,40},{64,... | collective-permute-start | bytes 1763336 | tf_op jit(solution)/shard_map/ppermute | solution.py:32
  40.5 0.9 bitcast_dynamic-update-slice_fusion.3
  42.2 8.5 %collective-permute-done.18 = bf16[328,896]{1,0:T(8,128)(2,1)S(1)} collective-permute-done((bf16[328,896]{1,0:T(8,128)(2,1)S(1)}, bf16[328,896]{1,0:T(8,128)(2,1)S(1)}, u32[]{:S(2)}, u32[]{:S(2)}) %collective-permute-start.18) | collective-permute-done | bytes 587808 | tf_op jit(solution)/shard_map/ppermute | solution.py:32
  50.8 0.9 bitcast_dynamic-update-slice_fusion.1
  51.6 2.5 %collective-permute-done.19 = bf16[328,896]{1,0:T(8,128)(2,1)S(1)} collective-permute-done((bf16[328,896]{1,0:T(8,128)(2,1)S(1)}, bf16[328,896]{1,0:T(8,128)(2,1)S(1)}, u32[]{:S(2)}, u32[]{:S(2)}) %collective-permute-start.19) | collective-permute-done | bytes 587808 | tf_op jit(solution)/shard_map/ppermute | solution.py:31
  54.2 0.9 bitcast_dynamic-update-slice_fusion.refs_8_.mine
  55.1 10.9 %collective-permute-start.20 = (bf16[7,328,896]{2,1,0:T(8,128)(2,1)}, bf16[7,328,896]{2,1,0:T(8,128)(2,1)}, u32[]{:S(2)}, u32[]{:S(2)}) collective-permute-start(bf16[7,328,896]{2,1,0:T(8,128)(2,1)} %bitcast_dynamic-update-slice_fusion.refs_8_.mine), channel_id=1, source_target_pairs={{0,8},{8,0},{16,24},{24,16},{32,40},{40,32},{48,56},{56,48},{64,72... | collective-permute-start | bytes 12343304 | tf_op jit(solution)/shard_map/ppermute | solution.py:46
  66.2 2.6 %collective-permute-start.1 = (bf16[320,640]{1,0:T(8,128)(2,1)S(1)}, bf16[320,640]{1,0:T(8,128)(2,1)S(1)}, u32[]{:S(2)}, u32[]{:S(2)}) collective-permute-start(bf16[320,640]{1,0:T(8,128)(2,1)S(1)} %get-tuple-element.20.refs_0_), channel_id=1, source_target_pairs={{0,7},{1,0},{2,1},{3,2},{4,3},{5,4},{6,5},{7,6},{8,15},{9,8},{10,9... | collective-permute-start | bytes 1228808 | tf_op jit(solution)/shard_map/ppermute | solution.py:32
  68.9 1.4 collective-permute-start
  70.7 7.6 %collective-permute-done.4.refs_7_ = bf16[320,640]{1,0:T(8,128)(2,1)S(1)} collective-permute-done((bf16[320,640]{1,0:T(8,128)(2,1)S(1)}, bf16[320,640]{1,0:T(8,128)(2,1)S(1)}, u32[]{:S(2)}, u32[]{:S(2)}) %collective-permute-start.4) | collective-permute-done | bytes 409632 | tf_op jit(solution)/shard_map/ppermute | solution.py:31
  78.5 1.2 fusion.2
  79.7 3.0 %collective-permute-start.2 = (bf16[320,640]{1,0:T(8,128)(2,1)S(1)}, bf16[320,640]{1,0:T(8,128)(2,1)S(1)}, u32[]{:S(2)}, u32[]{:S(2)}) collective-permute-start(bf16[320,640]{1,0:T(8,128)(2,1)S(1)} %collective-permute-done.1.refs_1_), channel_id=1, source_target_pairs={{0,7},{1,0},{2,1},{3,2},{4,3},{5,4},{6,5},{7,6},{8,15},{9,8},{10,9... | collective-permute-start | bytes 1228808 | tf_op jit(solution)/shard_map/ppermute | solution.py:32
  82.7 4.4 %collective-permute-done.refs_7_ = bf16[320,640]{1,0:T(8,128)(2,1)S(1)} collective-permute-done((bf16[320,640]{1,0:T(8,128)(2,1)S(1)}, bf16[320,640]{1,0:T(8,128)(2,1)S(1)}, u32[]{:S(2)}, u32[]{:S(2)}) %collective-permute-start) | collective-permute-done | bytes 409632 | tf_op jit(solution)/shard_map/ppermute | solution.py:31
  87.2 2.4 %collective-permute-start.9 = (bf16[320,640]{1,0:T(8,128)(2,1)S(1)}, bf16[320,640]{1,0:T(8,128)(2,1)S(1)}, u32[]{:S(2)}, u32[]{:S(2)}) collective-permute-start(bf16[320,640]{1,0:T(8,128)(2,1)S(1)} %collective-permute-done.8.refs_1_), channel_id=1, source_target_pairs={{0,7},{1,0},{2,1},{3,2},{4,3},{5,4},{6,5},{7,6},{8,15},{9,8},{10,9... | collective-permute-start | bytes 1228808 | tf_op jit(solution)/shard_map/ppermute | solution.py:32
  89.6 6.4 %collective-permute-done.5.refs_6_ = bf16[320,640]{1,0:T(8,128)(2,1)S(1)} collective-permute-done((bf16[320,640]{1,0:T(8,128)(2,1)S(1)}, bf16[320,640]{1,0:T(8,128)(2,1)S(1)}, u32[]{:S(2)}, u32[]{:S(2)}) %collective-permute-start.5) | collective-permute-done | bytes 409632 | tf_op jit(solution)/shard_map/ppermute | solution.py:31
  96.0 7.7 %collective-permute-done.9.refs_2_ = bf16[320,640]{1,0:T(8,128)(2,1)S(1)} collective-permute-done((bf16[320,640]{1,0:T(8,128)(2,1)S(1)}, bf16[320,640]{1,0:T(8,128)(2,1)S(1)}, u32[]{:S(2)}, u32[]{:S(2)}) %collective-permute-start.9) | collective-permute-done | bytes 409632 | tf_op jit(solution)/shard_map/ppermute | solution.py:32
  103.7 3.4 %collective-permute-start.3 = (bf16[320,640]{1,0:T(8,128)(2,1)S(1)}, bf16[320,640]{1,0:T(8,128)(2,1)S(1)}, u32[]{:S(2)}, u32[]{:S(2)}) collective-permute-start(bf16[320,640]{1,0:T(8,128)(2,1)S(1)} %collective-permute-done.2.refs_2_), channel_id=1, source_target_pairs={{0,7},{1,0},{2,1},{3,2},{4,3},{5,4},{6,5},{7,6},{8,15},{9,8},{10,9... | collective-permute-start | bytes 1228808 | tf_op jit(solution)/shard_map/ppermute | solution.py:32
  107.1 3.5 %collective-permute-done.21.refs_10_.mine_mid = bf16[328,896]{1,0:T(8,128)(2,1)S(1)} collective-permute-done((bf16[328,896]{1,0:T(8,128)(2,1)S(1)}, bf16[328,896]{1,0:T(8,128)(2,1)S(1)}, u32[]{:S(2)}, u32[]{:S(2)}) %collective-permute-start.21) | collective-permute-done | bytes 587808 | tf_op jit(solution)/shard_map/ppermute | solution.py:38
  110.7 2.2 %collective-permute-start.22 = (bf16[328,896]{1,0:T(8,128)(2,1)S(1)}, bf16[328,896]{1,0:T(8,128)(2,1)S(1)}, u32[]{:S(2)}, u32[]{:S(2)}) collective-permute-start(bf16[328,896]{1,0:T(8,128)(2,1)S(1)} %collective-permute-done.21.refs_10_.mine_mid), channel_id=1, source_target_pairs={{0,8},{8,0},{16,24},{24,16},{32,40},{40,32},{48,56},{56,48},{64,72... | collective-permute-start | bytes 1763336 | tf_op jit(solution)/shard_map/ppermute | solution.py:46
  113.5 1.3 collective-permute-done.3.refs_3_
  115.4 8.2 %collective-permute-done.10.refs_3_ = bf16[320,640]{1,0:T(8,128)(2,1)S(1)} collective-permute-done((bf16[320,640]{1,0:T(8,128)(2,1)S(1)}, bf16[320,640]{1,0:T(8,128)(2,1)S(1)}, u32[]{:S(2)}, u32[]{:S(2)}) %collective-permute-start.10) | collective-permute-done | bytes 409632 | tf_op jit(solution)/shard_map/ppermute | solution.py:32
  123.6 3.4 %collective-permute-start.11 = (bf16[320,640]{1,0:T(8,128)(2,1)S(1)}, bf16[320,640]{1,0:T(8,128)(2,1)S(1)}, u32[]{:S(2)}, u32[]{:S(2)}) collective-permute-start(bf16[320,640]{1,0:T(8,128)(2,1)S(1)} %collective-permute-done.10.refs_3_), channel_id=1, source_target_pairs={{0,7},{1,0},{2,1},{3,2},{4,3},{5,4},{6,5},{7,6},{8,15},{9,8},{10,9... | collective-permute-start | bytes 1228808 | tf_op jit(solution)/shard_map/ppermute | solution.py:40
  127.0 1.9 shard_map.95.x_a
  129.0 4.7 %collective-permute-done.13.refs_5_ = bf16[320,640]{1,0:T(8,128)(2,1)S(1)} collective-permute-done((bf16[320,640]{1,0:T(8,128)(2,1)S(1)}, bf16[320,640]{1,0:T(8,128)(2,1)S(1)}, u32[]{:S(2)}, u32[]{:S(2)}) %collective-permute-start.13) | collective-permute-done | bytes 409632 | tf_op jit(solution)/shard_map/ppermute | solution.py:31
  133.8 4.9 %shard_map.96 = (bf16[640,256]{1,0:T(8,128)(2,1)S(1)}, s32[16,128]{1,0:T(8,128)S(1)}, bf16[320,5120]{1,0:T(8,128)(2,1)S(1)}) custom-call(s32[4]{0:T(128)S(1)} %pad_add_fusion.place, bf16[320,5120]{1,0:T(8,128)(2,1)S(1)} %shard_map.95.x_a, bf16[320,640]{1,0:T(8,128)(2,1)S(1)} %get-tuple-element.21.refs_0_, ...), custom_call_target="tpu_custom_call" | custom-call | flops 1677721600 | bytes 13107200 | tf_op jit(solution)/shard_map/pallas_call | solution.py:177
  138.9 1.4 collective-permute-start.23
  140.3 5.0 %collective-permute-done.25 = bf16[640,256]{1,0:T(8,128)(2,1)S(1)} collective-permute-done((bf16[640,256]{1,0:T(8,128)(2,1)S(1)}, bf16[640,256]{1,0:T(8,128)(2,1)S(1)}, u32[]{:S(2)}, u32[]{:S(2)}) %collective-permute-start.25) | collective-permute-done | bytes 327712 | tf_op jit(solution)/shard_map/ppermute | solution.py:32
  145.2 1.5 collective-permute-start.26
  146.8 5.0 %collective-permute-done.26 = bf16[640,256]{1,0:T(8,128)(2,1)S(1)} collective-permute-done((bf16[640,256]{1,0:T(8,128)(2,1)S(1)}, bf16[640,256]{1,0:T(8,128)(2,1)S(1)}, u32[]{:S(2)}, u32[]{:S(2)}) %collective-permute-start.26) | collective-permute-done | bytes 327712 | tf_op jit(solution)/shard_map/ppermute | solution.py:32
  151.8 2.1 %collective-permute-start.28 = (bf16[640,256]{1,0:T(8,128)(2,1)S(1)}, bf16[640,256]{1,0:T(8,128)(2,1)S(1)}, u32[]{:S(2)}, u32[]{:S(2)}) collective-permute-start(bf16[640,256]{1,0:T(8,128)(2,1)S(1)} %collective-permute-done.26), channel_id=1, source_target_pairs={{0,112},{8,120},{16,0},{24,8},{32,16},{40,24},{48,32},{56,40},{64,... | collective-permute-start | bytes 983048 | tf_op jit(solution)/shard_map/ppermute | solution.py:32
  154.1 5.3 %collective-permute-done.28 = bf16[640,256]{1,0:T(8,128)(2,1)S(1)} collective-permute-done((bf16[640,256]{1,0:T(8,128)(2,1)S(1)}, bf16[640,256]{1,0:T(8,128)(2,1)S(1)}, u32[]{:S(2)}, u32[]{:S(2)}) %collective-permute-start.28) | collective-permute-done | bytes 327712 | tf_op jit(solution)/shard_map/ppermute | solution.py:32
  159.5 2.1 %collective-permute-done.29 = bf16[640,256]{1,0:T(8,128)(2,1)S(1)} collective-permute-done((bf16[640,256]{1,0:T(8,128)(2,1)S(1)}, bf16[640,256]{1,0:T(8,128)(2,1)S(1)}, u32[]{:S(2)}, u32[]{:S(2)}) %collective-permute-start.29) | collective-permute-done | bytes 327712 | tf_op jit(solution)/shard_map/ppermute | solution.py:31
  161.6 6.0 %collective-permute-start.30 = (bf16[4480,256]{1,0:T(8,128)(2,1)S(1)}, bf16[4480,256]{1,0:T(8,128)(2,1)S(1)}, u32[]{:S(2)}, u32[]{:S(2)}) collective-permute-start(bf16[4480,256]{1,0:T(8,128)(2,1)S(1)} %constant_dynamic-update-slice_fusion.mine), channel_id=1, source_target_pairs={{0,8},{8,0},{16,24},{24,16},{32,40},{40,32},{48,56},{56,48},{64,72... | collective-permute-start | bytes 6881288 | tf_op jit(solution)/shard_map/ppermute | solution.py:46
  167.6 1.9 collective-permute-start.24
  169.5 8.7 %shard_map.97.q_in = bf16[5,640,128]{2,1,0:T(8,128)(2,1)S(1)} custom-call(s32[4]{0:T(128)S(1)} %pad_add_fusion.place, bf16[320,5120]{1,0:T(8,128)(2,1)S(1)} %shard_map.95.x_a, bf16[320,5120]{1,0:T(8,128)(2,1)S(1)} %get-tuple-element.17.x_b, bf16[7,328,896]{2,1,0:T(8,128)(2,1)} %bitcast_dynamic-update-slice_fusion.refs_8_.mine, ...), custom_call_target="tpu_custom_call" | custom-call | flops 4194304000 | bytes 6553600 | tf_op jit(solution)/shard_map/pallas_call | solution.py:210
  178.4 5.9 %shard_map.98.refs_0_ = bf16[640,640]{1,0:T(8,128)(2,1)} custom-call(s32[9]{0:T(128)S(1)} %pad_add_fusion.1.info, bf16[5,640,128]{2,1,0:T(8,128)(2,1)S(1)} %shard_map.97.q_in, bf16[640,256]{1,0:T(8,128)(2,1)S(1)} %collective-permute-done.23.far, bf16[640,256]{1,0:T(8,128)(2,1)S(1)} %collective-permute-done.24.near, bf16[640,256]{1,0:T(8,128)(2,1)S(1)} %get-tuple-element.18.own), custom_call_target="tpu_custom_call" | custom-call | flops 4000000000 | bytes 4000000 | tf_op jit(solution)/shard_map/pallas_call | solution.py:340
  184.4 2.8 %collective-permute-done.31.mine_mid = bf16[640,256]{1,0:T(8,128)(2,1)S(1)} collective-permute-done((bf16[640,256]{1,0:T(8,128)(2,1)S(1)}, bf16[640,256]{1,0:T(8,128)(2,1)S(1)}, u32[]{:S(2)}, u32[]{:S(2)}) %collective-permute-start.31) | collective-permute-done | bytes 327712 | tf_op jit(solution)/shard_map/ppermute | solution.py:40
  187.2 1.4 collective-permute-start.32
  188.5 6.9 %shard_map.99.refs_0_ = bf16[640,640]{1,0:T(8,128)(2,1)} custom-call(s32[9]{0:T(128)S(1)} %pad_add_fusion.1.info, bf16[5,640,128]{2,1,0:T(8,128)(2,1)S(1)} %shard_map.97.q_in, bf16[640,256]{1,0:T(8,128)(2,1)S(1)} %collective-permute-done.23.far, bf16[640,256]{1,0:T(8,128)(2,1)S(1)} %collective-permute-done.24.near, ...), custom_call_target="tpu_custom_call", output_to_operand_aliasing={{}: (5, {})} | custom-call | flops 4000000000 | bytes 4000000 | tf_op jit(solution)/shard_map/pallas_call | solution.py:340
  195.5 2.5 %shard_map.100 = bf16[640,640]{1,0:T(8,128)(2,1)} custom-call(s32[9]{0:T(128)S(1)} %pad_add_fusion.1.info, bf16[5,640,128]{2,1,0:T(8,128)(2,1)S(1)} %shard_map.97.q_in, bf16[640,256]{1,0:T(8,128)(2,1)S(1)} %collective-permute-done.23.far, bf16[640,256]{1,0:T(8,128)(2,1)S(1)} %collective-permute-done.24.near, ...), custom_call_target="tpu_custom_call", output_to_operand_aliasing={{}: (5, {})} | custom-call | flops 2000000000 | bytes 4000000 | tf_op jit(solution)/shard_map/pallas_call | solution.py:340
  198.0 3.3 %shard_map.101 = bf16[32,128,256]{2,1,0:T(8,128)(2,1)} custom-call(s32[4]{0:T(128)S(1)} %pad_add_fusion.place, s32[16,128]{1,0:T(8,128)S(1)} %get-tuple-element.19.labels, s32[1,32]{1,0:T(1,128)S(1)} %copy-done, bf16[4480,256]{1,0:T(8,128)(2,1)S(1)} %constant_dynamic-update-slice_fusion.mine, bf16[4480,256]{1,0:T(8,128)(2,1)S(1)} %collective-permute-done.30.other, ...), custom_call_target="tpu_custom_call" | custom-call | tf_op jit(solution)/shard_map/pallas_call | solution.py:424
  (60 shorter events, 5.5 us)
Async XLA Ops:
  2.4 19.3 %collective-permute-start.14 = (bf16[328,896]{1,0:T(8,128)(2,1)S(1)}, bf16[328,896]{1,0:T(8,128)(2,1)S(1)}, u32[]{:S(2)}, u32[]{:S(2)}) collective-permute-start(bf16[328,896]{1,0:T(8,128)(2,1)S(1)} %fusion.1), channel_id=1, source_target_pairs={{0,112},{8,120},{16,0},{24,8},{32,16},{40,24},{48,32},{56,40},{64,... | collective-permute-start | bytes 1763336 | tf_op jit(solution)/shard_map/ppermute | solution.py:32
  15.0 12.2 %collective-permute-start.15 = (bf16[328,896]{1,0:T(8,128)(2,1)S(1)}, bf16[328,896]{1,0:T(8,128)(2,1)S(1)}, u32[]{:S(2)}, u32[]{:S(2)}) collective-permute-start(bf16[328,896]{1,0:T(8,128)(2,1)S(1)} %fusion.1), channel_id=1, source_target_pairs={{0,16},{8,24},{16,32},{24,40},{32,48},{40,56},{48,64},{56,72},{64,... | collective-permute-start | bytes 1763336 | tf_op jit(solution)/shard_map/ppermute | solution.py:31
  21.8 14.5 %collective-permute-start.16 = (bf16[328,896]{1,0:T(8,128)(2,1)S(1)}, bf16[328,896]{1,0:T(8,128)(2,1)S(1)}, u32[]{:S(2)}, u32[]{:S(2)}) collective-permute-start(bf16[328,896]{1,0:T(8,128)(2,1)S(1)} %collective-permute-done.14), channel_id=1, source_target_pairs={{0,112},{8,120},{16,0},{24,8},{32,16},{40,24},{48,32},{56,40},{64,... | collective-permute-start | bytes 1763336 | tf_op jit(solution)/shard_map/ppermute | solution.py:32
  27.2 13.1 %collective-permute-start.17 = (bf16[328,896]{1,0:T(8,128)(2,1)S(1)}, bf16[328,896]{1,0:T(8,128)(2,1)S(1)}, u32[]{:S(2)}, u32[]{:S(2)}) collective-permute-start(bf16[328,896]{1,0:T(8,128)(2,1)S(1)} %collective-permute-done.15), channel_id=1, source_target_pairs={{0,16},{8,24},{16,32},{24,40},{32,48},{40,56},{48,64},{56,72},{64,... | collective-permute-start | bytes 1763336 | tf_op jit(solution)/shard_map/ppermute | solution.py:31
  36.3 14.5 %collective-permute-start.18 = (bf16[328,896]{1,0:T(8,128)(2,1)S(1)}, bf16[328,896]{1,0:T(8,128)(2,1)S(1)}, u32[]{:S(2)}, u32[]{:S(2)}) collective-permute-start(bf16[328,896]{1,0:T(8,128)(2,1)S(1)} %collective-permute-done.16), channel_id=1, source_target_pairs={{0,112},{8,120},{16,0},{24,8},{32,16},{40,24},{48,32},{56,40},{64,... | collective-permute-start | bytes 1763336 | tf_op jit(solution)/shard_map/ppermute | solution.py:32
  40.2 25.7 %copy-start.1 = (bf16[640,640]{1,0:T(8,128)(2,1)S(1)}, bf16[640,640]{1,0:T(8,128)(2,1)}, u32[]{:S(2)}) copy-start(bf16[640,640]{1,0:T(8,128)(2,1)} %param.8) | copy-start | bytes 2457604
  40.2 13.9 %collective-permute-start.19 = (bf16[328,896]{1,0:T(8,128)(2,1)S(1)}, bf16[328,896]{1,0:T(8,128)(2,1)S(1)}, u32[]{:S(2)}, u32[]{:S(2)}) collective-permute-start(bf16[328,896]{1,0:T(8,128)(2,1)S(1)} %collective-permute-done.17), channel_id=1, source_target_pairs={{0,16},{8,24},{16,32},{24,40},{32,48},{40,56},{48,64},{56,72},{64,... | collective-permute-start | bytes 1763336 | tf_op jit(solution)/shard_map/ppermute | solution.py:31
  42.2 28.1 %copy-start.3 = (s32[8]{0:T(128)S(1)}, s32[8]{0:T(128)}, u32[]{:S(2)}) copy-start(s32[8]{0:T(128)} %param.13) | copy-start | bytes 100
  42.2 28.4 %copy-start.2 = (bf16[5120]{0:T(1024)(128)(2,1)S(1)}, bf16[5120]{0:T(1024)(128)(2,1)}, u32[]{:S(2)}) copy-start(bf16[5120]{0:T(1024)(128)(2,1)} %param.9) | copy-start | bytes 30724
  55.1 78.7 %collective-permute-start.20 = (bf16[7,328,896]{2,1,0:T(8,128)(2,1)}, bf16[7,328,896]{2,1,0:T(8,128)(2,1)}, u32[]{:S(2)}, u32[]{:S(2)}) collective-permute-start(bf16[7,328,896]{2,1,0:T(8,128)(2,1)} %bitcast_dynamic-update-slice_fusion.refs_8_.mine), channel_id=1, source_target_pairs={{0,8},{8,0},{16,24},{24,16},{32,40},{40,32},{48,56},{56,48},{64,72... | collective-permute-start | bytes 12343304 | tf_op jit(solution)/shard_map/ppermute | solution.py:46
  66.0 12.3 %collective-permute-start.4 = (bf16[320,640]{1,0:T(8,128)(2,1)S(1)}, bf16[320,640]{1,0:T(8,128)(2,1)S(1)}, u32[]{:S(2)}, u32[]{:S(2)}) collective-permute-start(bf16[320,640]{1,0:T(8,128)(2,1)S(1)} %get-tuple-element.20.refs_0_), channel_id=1, source_target_pairs={{0,1},{1,2},{2,3},{3,4},{4,5},{5,6},{6,7},{7,0},{8,9},{9,10},{10,1... | collective-permute-start | bytes 1228808 | tf_op jit(solution)/shard_map/ppermute | solution.py:31
  66.2 13.5 %collective-permute-start.1 = (bf16[320,640]{1,0:T(8,128)(2,1)S(1)}, bf16[320,640]{1,0:T(8,128)(2,1)S(1)}, u32[]{:S(2)}, u32[]{:S(2)}) collective-permute-start(bf16[320,640]{1,0:T(8,128)(2,1)S(1)} %get-tuple-element.20.refs_0_), channel_id=1, source_target_pairs={{0,7},{1,0},{2,1},{3,2},{4,3},{5,4},{6,5},{7,6},{8,15},{9,8},{10,9... | collective-permute-start | bytes 1228808 | tf_op jit(solution)/shard_map/ppermute | solution.py:32
  68.8 18.3 %collective-permute-start.8 = (bf16[320,640]{1,0:T(8,128)(2,1)S(1)}, bf16[320,640]{1,0:T(8,128)(2,1)S(1)}, u32[]{:S(2)}, u32[]{:S(2)}) collective-permute-start(bf16[320,640]{1,0:T(8,128)(2,1)S(1)} %get-tuple-element.21.refs_0_), channel_id=1, source_target_pairs={{0,7},{1,0},{2,1},{3,2},{4,3},{5,4},{6,5},{7,6},{8,15},{9,8},{10,9... | collective-permute-start | bytes 1228808 | tf_op jit(solution)/shard_map/ppermute | solution.py:32
  68.9 18.3 %collective-permute-start = (bf16[320,640]{1,0:T(8,128)(2,1)S(1)}, bf16[320,640]{1,0:T(8,128)(2,1)S(1)}, u32[]{:S(2)}, u32[]{:S(2)}) collective-permute-start(bf16[320,640]{1,0:T(8,128)(2,1)S(1)} %get-tuple-element.21.refs_0_), channel_id=1, source_target_pairs={{0,1},{1,2},{2,3},{3,4},{4,5},{5,6},{6,7},{7,0},{8,9},{9,10},{10,1... | collective-permute-start | bytes 1228808 | tf_op jit(solution)/shard_map/ppermute | solution.py:31
  78.4 17.6 %collective-permute-start.5 = (bf16[320,640]{1,0:T(8,128)(2,1)S(1)}, bf16[320,640]{1,0:T(8,128)(2,1)S(1)}, u32[]{:S(2)}, u32[]{:S(2)}) collective-permute-start(bf16[320,640]{1,0:T(8,128)(2,1)S(1)} %collective-permute-done.4.refs_7_), channel_id=1, source_target_pairs={{0,1},{1,2},{2,3},{3,4},{4,5},{5,6},{6,7},{7,0},{8,9},{9,10},{10,1... | collective-permute-start | bytes 1228808 | tf_op jit(solution)/shard_map/ppermute | solution.py:31
  79.7 16.2 %collective-permute-start.2 = (bf16[320,640]{1,0:T(8,128)(2,1)S(1)}, bf16[320,640]{1,0:T(8,128)(2,1)S(1)}, u32[]{:S(2)}, u32[]{:S(2)}) collective-permute-start(bf16[320,640]{1,0:T(8,128)(2,1)S(1)} %collective-permute-done.1.refs_1_), channel_id=1, source_target_pairs={{0,7},{1,0},{2,1},{3,2},{4,3},{5,4},{6,5},{7,6},{8,15},{9,8},{10,9... | collective-permute-start | bytes 1228808 | tf_op jit(solution)/shard_map/ppermute | solution.py:32
  87.2 16.5 %collective-permute-start.9 = (bf16[320,640]{1,0:T(8,128)(2,1)S(1)}, bf16[320,640]{1,0:T(8,128)(2,1)S(1)}, u32[]{:S(2)}, u32[]{:S(2)}) collective-permute-start(bf16[320,640]{1,0:T(8,128)(2,1)S(1)} %collective-permute-done.8.refs_1_), channel_id=1, source_target_pairs={{0,7},{1,0},{2,1},{3,2},{4,3},{5,4},{6,5},{7,6},{8,15},{9,8},{10,9... | collective-permute-start | bytes 1228808 | tf_op jit(solution)/shard_map/ppermute | solution.py:32
  89.6 17.6 %collective-permute-start.12 = (bf16[320,640]{1,0:T(8,128)(2,1)S(1)}, bf16[320,640]{1,0:T(8,128)(2,1)S(1)}, u32[]{:S(2)}, u32[]{:S(2)}) collective-permute-start(bf16[320,640]{1,0:T(8,128)(2,1)S(1)} %collective-permute-done.refs_7_), channel_id=1, source_target_pairs={{0,1},{1,2},{2,3},{3,4},{4,5},{5,6},{6,7},{7,0},{8,9},{9,10},{10,1... | collective-permute-start | bytes 1228808 | tf_op jit(solution)/shard_map/ppermute | solution.py:31
  95.9 14.7 %collective-permute-start.21 = (bf16[328,896]{1,0:T(8,128)(2,1)S(1)}, bf16[328,896]{1,0:T(8,128)(2,1)S(1)}, u32[]{:S(2)}, u32[]{:S(2)}) collective-permute-start(bf16[328,896]{1,0:T(8,128)(2,1)S(1)} %collective-permute-done.19), channel_id=1, source_target_pairs={{0,16},{8,24},{16,32},{24,40},{32,48},{40,56},{48,64},{56,72},{64,... | collective-permute-start | bytes 1763336 | tf_op jit(solution)/shard_map/ppermute | solution.py:38
  95.9 17.5 %collective-permute-start.6 = (bf16[320,640]{1,0:T(8,128)(2,1)S(1)}, bf16[320,640]{1,0:T(8,128)(2,1)S(1)}, u32[]{:S(2)}, u32[]{:S(2)}) collective-permute-start(bf16[320,640]{1,0:T(8,128)(2,1)S(1)} %collective-permute-done.5.refs_6_), channel_id=1, source_target_pairs={{0,1},{1,2},{2,3},{3,4},{4,5},{5,6},{6,7},{7,0},{8,9},{9,10},{10,1... | collective-permute-start | bytes 1228808 | tf_op jit(solution)/shard_map/ppermute | solution.py:31
  103.7 11.1 %collective-permute-start.3 = (bf16[320,640]{1,0:T(8,128)(2,1)S(1)}, bf16[320,640]{1,0:T(8,128)(2,1)S(1)}, u32[]{:S(2)}, u32[]{:S(2)}) collective-permute-start(bf16[320,640]{1,0:T(8,128)(2,1)S(1)} %collective-permute-done.2.refs_2_), channel_id=1, source_target_pairs={{0,7},{1,0},{2,1},{3,2},{4,3},{5,4},{6,5},{7,6},{8,15},{9,8},{10,9... | collective-permute-start | bytes 1228808 | tf_op jit(solution)/shard_map/ppermute | solution.py:32
  107.1 16.5 %collective-permute-start.10 = (bf16[320,640]{1,0:T(8,128)(2,1)S(1)}, bf16[320,640]{1,0:T(8,128)(2,1)S(1)}, u32[]{:S(2)}, u32[]{:S(2)}) collective-permute-start(bf16[320,640]{1,0:T(8,128)(2,1)S(1)} %collective-permute-done.9.refs_2_), channel_id=1, source_target_pairs={{0,7},{1,0},{2,1},{3,2},{4,3},{5,4},{6,5},{7,6},{8,15},{9,8},{10,9... | collective-permute-start | bytes 1228808 | tf_op jit(solution)/shard_map/ppermute | solution.py:32
  110.7 23.1 %collective-permute-start.22 = (bf16[328,896]{1,0:T(8,128)(2,1)S(1)}, bf16[328,896]{1,0:T(8,128)(2,1)S(1)}, u32[]{:S(2)}, u32[]{:S(2)}) collective-permute-start(bf16[328,896]{1,0:T(8,128)(2,1)S(1)} %collective-permute-done.21.refs_10_.mine_mid), channel_id=1, source_target_pairs={{0,8},{8,0},{16,24},{24,16},{32,40},{40,32},{48,56},{56,48},{64,72... | collective-permute-start | bytes 1763336 | tf_op jit(solution)/shard_map/ppermute | solution.py:46
  113.5 13.5 %collective-permute-start.7 = (bf16[320,640]{1,0:T(8,128)(2,1)S(1)}, bf16[320,640]{1,0:T(8,128)(2,1)S(1)}, u32[]{:S(2)}, u32[]{:S(2)}) collective-permute-start(bf16[320,640]{1,0:T(8,128)(2,1)S(1)} %collective-permute-done.6.refs_5_), channel_id=1, source_target_pairs={{0,1},{1,2},{2,3},{3,4},{4,5},{5,6},{6,7},{7,0},{8,9},{9,10},{10,1... | collective-permute-start | bytes 1228808 | tf_op jit(solution)/shard_map/ppermute | solution.py:38
  114.8 18.8 %collective-permute-start.13 = (bf16[320,640]{1,0:T(8,128)(2,1)S(1)}, bf16[320,640]{1,0:T(8,128)(2,1)S(1)}, u32[]{:S(2)}, u32[]{:S(2)}) collective-permute-start(bf16[320,640]{1,0:T(8,128)(2,1)S(1)} %collective-permute-done.12.refs_6_), channel_id=1, source_target_pairs={{0,1},{1,2},{2,3},{3,4},{4,5},{5,6},{6,7},{7,0},{8,9},{9,10},{10,1... | collective-permute-start | bytes 1228808 | tf_op jit(solution)/shard_map/ppermute | solution.py:31
  123.6 10.2 %collective-permute-start.11 = (bf16[320,640]{1,0:T(8,128)(2,1)S(1)}, bf16[320,640]{1,0:T(8,128)(2,1)S(1)}, u32[]{:S(2)}, u32[]{:S(2)}) collective-permute-start(bf16[320,640]{1,0:T(8,128)(2,1)S(1)} %collective-permute-done.10.refs_3_), channel_id=1, source_target_pairs={{0,7},{1,0},{2,1},{3,2},{4,3},{5,4},{6,5},{7,6},{8,15},{9,8},{10,9... | collective-permute-start | bytes 1228808 | tf_op jit(solution)/shard_map/ppermute | solution.py:40
  138.7 6.5 %collective-permute-start.25 = (bf16[640,256]{1,0:T(8,128)(2,1)S(1)}, bf16[640,256]{1,0:T(8,128)(2,1)S(1)}, u32[]{:S(2)}, u32[]{:S(2)}) collective-permute-start(bf16[640,256]{1,0:T(8,128)(2,1)S(1)} %get-tuple-element.18.own), channel_id=1, source_target_pairs={{0,112},{8,120},{16,0},{24,8},{32,16},{40,24},{48,32},{56,40},{64,... | collective-permute-start | bytes 983048 | tf_op jit(solution)/shard_map/ppermute | solution.py:32
  138.9 7.9 %collective-permute-start.23 = (bf16[640,256]{1,0:T(8,128)(2,1)S(1)}, bf16[640,256]{1,0:T(8,128)(2,1)S(1)}, u32[]{:S(2)}, u32[]{:S(2)}) collective-permute-start(bf16[640,256]{1,0:T(8,128)(2,1)S(1)} %get-tuple-element.18.own), channel_id=1, source_target_pairs={{0,16},{8,24},{16,32},{24,40},{32,48},{40,56},{48,64},{56,72},{64,... | collective-permute-start | bytes 983048 | tf_op jit(solution)/shard_map/ppermute | solution.py:31
  145.2 6.5 %collective-permute-start.26 = (bf16[640,256]{1,0:T(8,128)(2,1)S(1)}, bf16[640,256]{1,0:T(8,128)(2,1)S(1)}, u32[]{:S(2)}, u32[]{:S(2)}) collective-permute-start(bf16[640,256]{1,0:T(8,128)(2,1)S(1)} %collective-permute-done.25), channel_id=1, source_target_pairs={{0,112},{8,120},{16,0},{24,8},{32,16},{40,24},{48,32},{56,40},{64,... | collective-permute-start | bytes 983048 | tf_op jit(solution)/shard_map/ppermute | solution.py:32
  146.8 7.2 %collective-permute-start.27 = (bf16[640,256]{1,0:T(8,128)(2,1)S(1)}, bf16[640,256]{1,0:T(8,128)(2,1)S(1)}, u32[]{:S(2)}, u32[]{:S(2)}) collective-permute-start(bf16[640,256]{1,0:T(8,128)(2,1)S(1)} %collective-permute-done.23.far), channel_id=1, source_target_pairs={{0,16},{8,24},{16,32},{24,40},{32,48},{40,56},{48,64},{56,72},{64,... | collective-permute-start | bytes 983048 | tf_op jit(solution)/shard_map/ppermute | solution.py:31
  151.8 7.7 %collective-permute-start.28 = (bf16[640,256]{1,0:T(8,128)(2,1)S(1)}, bf16[640,256]{1,0:T(8,128)(2,1)S(1)}, u32[]{:S(2)}, u32[]{:S(2)}) collective-permute-start(bf16[640,256]{1,0:T(8,128)(2,1)S(1)} %collective-permute-done.26), channel_id=1, source_target_pairs={{0,112},{8,120},{16,0},{24,8},{32,16},{40,24},{48,32},{56,40},{64,... | collective-permute-start | bytes 983048 | tf_op jit(solution)/shard_map/ppermute | solution.py:32
  153.9 7.6 %collective-permute-start.29 = (bf16[640,256]{1,0:T(8,128)(2,1)S(1)}, bf16[640,256]{1,0:T(8,128)(2,1)S(1)}, u32[]{:S(2)}, u32[]{:S(2)}) collective-permute-start(bf16[640,256]{1,0:T(8,128)(2,1)S(1)} %collective-permute-done.27), channel_id=1, source_target_pairs={{0,16},{8,24},{16,32},{24,40},{32,48},{40,56},{48,64},{56,72},{64,... | collective-permute-start | bytes 983048 | tf_op jit(solution)/shard_map/ppermute | solution.py:31
  161.6 36.4 %collective-permute-start.30 = (bf16[4480,256]{1,0:T(8,128)(2,1)S(1)}, bf16[4480,256]{1,0:T(8,128)(2,1)S(1)}, u32[]{:S(2)}, u32[]{:S(2)}) collective-permute-start(bf16[4480,256]{1,0:T(8,128)(2,1)S(1)} %constant_dynamic-update-slice_fusion.mine), channel_id=1, source_target_pairs={{0,8},{8,0},{16,24},{24,16},{32,40},{40,32},{48,56},{56,48},{64,72... | collective-permute-start | bytes 6881288 | tf_op jit(solution)/shard_map/ppermute | solution.py:46
  167.6 10.8 %collective-permute-start.24 = (bf16[640,256]{1,0:T(8,128)(2,1)S(1)}, bf16[640,256]{1,0:T(8,128)(2,1)S(1)}, u32[]{:S(2)}, u32[]{:S(2)}) collective-permute-start(bf16[640,256]{1,0:T(8,128)(2,1)S(1)} %get-tuple-element.18.own), channel_id=1, source_target_pairs={{0,8},{8,16},{16,24},{24,32},{32,40},{40,48},{48,56},{56,64},{64,7... | collective-permute-start | bytes 983048 | tf_op jit(solution)/shard_map/ppermute | solution.py:485
  178.3 8.9 %collective-permute-start.31 = (bf16[640,256]{1,0:T(8,128)(2,1)S(1)}, bf16[640,256]{1,0:T(8,128)(2,1)S(1)}, u32[]{:S(2)}, u32[]{:S(2)}) collective-permute-start(bf16[640,256]{1,0:T(8,128)(2,1)S(1)} %collective-permute-done.28), channel_id=1, source_target_pairs={{0,112},{8,120},{16,0},{24,8},{32,16},{40,24},{48,32},{56,40},{64,... | collective-permute-start | bytes 983048 | tf_op jit(solution)/shard_map/ppermute | solution.py:40
  187.2 10.8 %collective-permute-start.32 = (bf16[640,256]{1,0:T(8,128)(2,1)S(1)}, bf16[640,256]{1,0:T(8,128)(2,1)S(1)}, u32[]{:S(2)}, u32[]{:S(2)}) collective-permute-start(bf16[640,256]{1,0:T(8,128)(2,1)S(1)} %collective-permute-done.31.mine_mid), channel_id=1, source_target_pairs={{0,8},{8,0},{16,24},{24,16},{32,40},{40,32},{48,56},{56,48},{64,72... | collective-permute-start | bytes 983048 | tf_op jit(solution)/shard_map/ppermute | solution.py:46
  195.5 2.6 %copy-start = (s32[1,32]{1,0:T(1,128)S(1)}, s32[1,32]{1,0:T(1,128)}, u32[]{:S(2)}) copy-start(s32[1,32]{1,0:T(1,128)} %table.1) | copy-start | bytes 388
where the time goes:
time: 204 us; the launch traced here: 202 us
  waiting for transfers between devices  89 us (44%)
  starting transfers between devices  66.1 us (32%)
  Pallas kernels  34.2 us (17%)
  other arithmetic  5.57 us (3%)
  local copies, waits for them, and re-layouts  5.5 us (3%)
    ppermute x12, waiting for transfers between devices, ring(): down = lax.ppermute(down, axis, back)  54.1 us
    ppermute x12, starting transfers between devices, ring(): down = lax.ppermute(down, axis, back)  36.3 us
    ppermute x12, waiting for transfers between devices, ring(): up = lax.ppermute(up, axis, ahead)  28.4 us
    ppermute x4, starting transfers between devices, swap(): return lax.ppermute(block, axis, [(i, i ^ 1) for i in range(size)])  20.4 us
    pallas_call x3, Pallas kernels, attend(): pl.pallas_call(functools.partial(attend_kernel, lo=lo, hi=hi), out_shape=...  15.4 us
    pallas_call x1, Pallas kernels, project_queries(): pl.pallas_call(functools.partial(queries_kernel, count=count, feat=feat,...  8.74 us
    pallas_call x1, Pallas kernels, project_keys(): pl.pallas_call(functools.partial(keys_kernel, count=count, feat=feat, lo=...  4.88 us
    unnamed x19, local copies, waits for them, and re-layouts  4.47 us
  transfers between devices with their start and end apart: 33, of which 19 were waited for; matrix products, arithmetic and copies ran while one was open for 4% of the time, Pallas kernels for 13%

commit v1 on v0

--- a/solution.py
+++ b/solution.py
@@ -449,12 +449,12 @@
     starts = (jnp.cumsum(prompt_blocks) - prompt_blocks) * BLOCK
     start_of = jnp.max(jnp.where(token_rows[:, None] >= starts[None, :], starts[None, :], 0), axis=1)
     offsets = token_rows - start_of
-    lane = jnp.arange(HD, dtype=jnp.int32)
-    freq_index = lax.rem(lane, HD // 2).astype(jnp.float32)
+    freq_index = jnp.arange(HD // 2, dtype=jnp.float32)
     inverse = jnp.exp(freq_index * (-2.0 * math.log(THETA) / HD))
     angles = offsets.astype(jnp.float32)[:, None] * inverse[None, :]
-    cos = jnp.cos(angles)
-    sin = jnp.sin(angles) * jnp.where(lane < HD // 2, -1.0, 1.0)[None, :]
+    cosine, sine = jnp.cos(angles), jnp.sin(angles)
+    cos = jnp.concatenate([cosine, cosine], axis=1)
+    sin = jnp.concatenate([-sine, sine], axis=1)
     gain = norm_gain.astype(jnp.float32)
     gain = lax.dynamic_slice_in_dim(
         jnp.concatenate([gain, gain]), lax.axis_index("tp") * feat, n_tp * feat

time: 204 us -> 205 us (level)
  waiting for transfers between devices: 89 us -> 86.8 us
  other arithmetic: 5.57 us -> 7.74 us
    ppermute x12, waiting for transfers between devices: 28.4 us -> 26.2 us  [ring(): up = lax.ppermute(up, axis, ahead)]
    unnamed x19 -> x21, local copies, waits for them, and re-layouts: 4.47 us -> 4.51 us
  transfers between devices with their start and end apart: 33 -> 33, of which waited for: 19 -> 19; matrix products, arithmetic and copies ran while one was open for 4% -> 5% of each run, Pallas kernels for 13% -> 13%
where the time goes in v1:
time: 205 us; the launch traced here: 202 us
  waiting for transfers between devices  86.8 us (42%)
  starting transfers between devices  65.9 us (32%)
  Pallas kernels  34.8 us (17%)
  other arithmetic  7.74 us (4%)
  local copies, waits for them, and re-layouts  5.59 us (3%)
    ppermute x12, waiting for transfers between devices, ring(): down = lax.ppermute(down, axis, back)  54.1 us
    ppermute x12, starting transfers between devices, ring(): down = lax.ppermute(down, axis, back)  36.1 us
    ppermute x12, waiting for transfers between devices, ring(): up = lax.ppermute(up, axis, ahead)  26.2 us
    ppermute x4, starting transfers between devices, swap(): return lax.ppermute(block, axis, [(i, i ^ 1) for i in range(size)])  20.4 us
    pallas_call x3, Pallas kernels, attend(): pl.pallas_call(functools.partial(attend_kernel, lo=lo, hi=hi), out_shape=...  15.8 us
    pallas_call x1, Pallas kernels, project_queries(): pl.pallas_call(functools.partial(queries_kernel, count=count, feat=feat,...  8.8 us
    pallas_call x1, Pallas kernels, project_keys(): pl.pallas_call(functools.partial(keys_kernel, count=count, feat=feat, lo=...  4.87 us
    unnamed x21, local copies, waits for them, and re-layouts  4.51 us
  transfers between devices with their start and end apart: 33, of which 19 were waited for; matrix products, arithmetic and copies ran while one was open for 5% of the time, Pallas kernels for 13%

profile of v1, /device:TPU:513, one launch (start us, length us, event | category | flops | bytes accessed | tf_op | source)
XLA Modules:
  0.0 201.9 jit_solution(7837465163415653767)
XLA Ops:
  1.3 1.1 fusion.1
  2.4 12.5 %collective-permute-start.14 = (bf16[328,896]{1,0:T(8,128)(2,1)S(1)}, bf16[328,896]{1,0:T(8,128)(2,1)S(1)}, u32[]{:S(2)}, u32[]{:S(2)}) collective-permute-start(bf16[328,896]{1,0:T(8,128)(2,1)S(1)} %fusion.1), channel_id=1, source_target_pairs={{0,112},{8,120},{16,0},{24,8},{32,16},{40,24},{48,32},{56,40},{64,... | collective-permute-start | bytes 1763336 | tf_op jit(solution)/shard_map/ppermute | solution.py:32
  15.0 6.8 %collective-permute-done.14 = bf16[328,896]{1,0:T(8,128)(2,1)S(1)} collective-permute-done((bf16[328,896]{1,0:T(8,128)(2,1)S(1)}, bf16[328,896]{1,0:T(8,128)(2,1)S(1)}, u32[]{:S(2)}, u32[]{:S(2)}) %collective-permute-start.14) | collective-permute-done | bytes 587808 | tf_op jit(solution)/shard_map/ppermute | solution.py:32
  21.8 5.4 %collective-permute-start.16 = (bf16[328,896]{1,0:T(8,128)(2,1)S(1)}, bf16[328,896]{1,0:T(8,128)(2,1)S(1)}, u32[]{:S(2)}, u32[]{:S(2)}) collective-permute-start(bf16[328,896]{1,0:T(8,128)(2,1)S(1)} %collective-permute-done.14), channel_id=1, source_target_pairs={{0,112},{8,120},{16,0},{24,8},{32,16},{40,24},{48,32},{56,40},{64,... | collective-permute-start | bytes 1763336 | tf_op jit(solution)/shard_map/ppermute | solution.py:32
  27.2 2.0 bitcast_dynamic-update-slice_fusion.6
  29.1 0.9 bitcast_dynamic-update-slice_fusion.5
  30.0 6.2 %collective-permute-done.16 = bf16[328,896]{1,0:T(8,128)(2,1)S(1)} collective-permute-done((bf16[328,896]{1,0:T(8,128)(2,1)S(1)}, bf16[328,896]{1,0:T(8,128)(2,1)S(1)}, u32[]{:S(2)}, u32[]{:S(2)}) %collective-permute-start.16) | collective-permute-done | bytes 587808 | tf_op jit(solution)/shard_map/ppermute | solution.py:32
  36.3 3.1 %collective-permute-start.18 = (bf16[328,896]{1,0:T(8,128)(2,1)S(1)}, bf16[328,896]{1,0:T(8,128)(2,1)S(1)}, u32[]{:S(2)}, u32[]{:S(2)}) collective-permute-start(bf16[328,896]{1,0:T(8,128)(2,1)S(1)} %collective-permute-done.16), channel_id=1, source_target_pairs={{0,112},{8,120},{16,0},{24,8},{32,16},{40,24},{48,32},{56,40},{64,... | collective-permute-start | bytes 1763336 | tf_op jit(solution)/shard_map/ppermute | solution.py:32
  40.5 0.9 bitcast_dynamic-update-slice_fusion.3
  42.2 8.5 %collective-permute-done.18 = bf16[328,896]{1,0:T(8,128)(2,1)S(1)} collective-permute-done((bf16[328,896]{1,0:T(8,128)(2,1)S(1)}, bf16[328,896]{1,0:T(8,128)(2,1)S(1)}, u32[]{:S(2)}, u32[]{:S(2)}) %collective-permute-start.18) | collective-permute-done | bytes 587808 | tf_op jit(solution)/shard_map/ppermute | solution.py:32
  51.6 2.5 %collective-permute-done.19 = bf16[328,896]{1,0:T(8,128)(2,1)S(1)} collective-permute-done((bf16[328,896]{1,0:T(8,128)(2,1)S(1)}, bf16[328,896]{1,0:T(8,128)(2,1)S(1)}, u32[]{:S(2)}, u32[]{:S(2)}) %collective-permute-start.19) | collective-permute-done | bytes 587808 | tf_op jit(solution)/shard_map/ppermute | solution.py:31
  54.2 1.0 bitcast_dynamic-update-slice_fusion.refs_8_.mine
  55.1 10.9 %collective-permute-start.20 = (bf16[7,328,896]{2,1,0:T(8,128)(2,1)}, bf16[7,328,896]{2,1,0:T(8,128)(2,1)}, u32[]{:S(2)}, u32[]{:S(2)}) collective-permute-start(bf16[7,328,896]{2,1,0:T(8,128)(2,1)} %bitcast_dynamic-update-slice_fusion.refs_8_.mine), channel_id=1, source_target_pairs={{0,8},{8,0},{16,24},{24,16},{32,40},{40,32},{48,56},{56,48},{64,72... | collective-permute-start | bytes 12343304 | tf_op jit(solution)/shard_map/ppermute | solution.py:46
  66.3 2.6 %collective-permute-start.1 = (bf16[320,640]{1,0:T(8,128)(2,1)S(1)}, bf16[320,640]{1,0:T(8,128)(2,1)S(1)}, u32[]{:S(2)}, u32[]{:S(2)}) collective-permute-start(bf16[320,640]{1,0:T(8,128)(2,1)S(1)} %get-tuple-element.20.refs_0_), channel_id=1, source_target_pairs={{0,7},{1,0},{2,1},{3,2},{4,3},{5,4},{6,5},{7,6},{8,15},{9,8},{10,9... | collective-permute-start | bytes 1228808 | tf_op jit(solution)/shard_map/ppermute | solution.py:32
  69.0 1.4 collective-permute-start
  70.7 2.0 fusion.2
  72.7 5.8 %collective-permute-done.4.refs_7_ = bf16[320,640]{1,0:T(8,128)(2,1)S(1)} collective-permute-done((bf16[320,640]{1,0:T(8,128)(2,1)S(1)}, bf16[320,640]{1,0:T(8,128)(2,1)S(1)}, u32[]{:S(2)}, u32[]{:S(2)}) %collective-permute-start.4) | collective-permute-done | bytes 409632 | tf_op jit(solution)/shard_map/ppermute | solution.py:31
  78.7 1.4 pad_maximum_fusion
  80.1 2.8 %collective-permute-start.2 = (bf16[320,640]{1,0:T(8,128)(2,1)S(1)}, bf16[320,640]{1,0:T(8,128)(2,1)S(1)}, u32[]{:S(2)}, u32[]{:S(2)}) collective-permute-start(bf16[320,640]{1,0:T(8,128)(2,1)S(1)} %collective-permute-done.1.refs_1_), channel_id=1, source_target_pairs={{0,7},{1,0},{2,1},{3,2},{4,3},{5,4},{6,5},{7,6},{8,15},{9,8},{10,9... | collective-permute-start | bytes 1228808 | tf_op jit(solution)/shard_map/ppermute | solution.py:32
  82.9 4.3 %collective-permute-done.refs_7_ = bf16[320,640]{1,0:T(8,128)(2,1)S(1)} collective-permute-done((bf16[320,640]{1,0:T(8,128)(2,1)S(1)}, bf16[320,640]{1,0:T(8,128)(2,1)S(1)}, u32[]{:S(2)}, u32[]{:S(2)}) %collective-permute-start) | collective-permute-done | bytes 409632 | tf_op jit(solution)/shard_map/ppermute | solution.py:31
  87.2 2.4 %collective-permute-start.9 = (bf16[320,640]{1,0:T(8,128)(2,1)S(1)}, bf16[320,640]{1,0:T(8,128)(2,1)S(1)}, u32[]{:S(2)}, u32[]{:S(2)}) collective-permute-start(bf16[320,640]{1,0:T(8,128)(2,1)S(1)} %collective-permute-done.8.refs_1_), channel_id=1, source_target_pairs={{0,7},{1,0},{2,1},{3,2},{4,3},{5,4},{6,5},{7,6},{8,15},{9,8},{10,9... | collective-permute-start | bytes 1228808 | tf_op jit(solution)/shard_map/ppermute | solution.py:32
  89.6 6.4 %collective-permute-done.5.refs_6_ = bf16[320,640]{1,0:T(8,128)(2,1)S(1)} collective-permute-done((bf16[320,640]{1,0:T(8,128)(2,1)S(1)}, bf16[320,640]{1,0:T(8,128)(2,1)S(1)}, u32[]{:S(2)}, u32[]{:S(2)}) %collective-permute-start.5) | collective-permute-done | bytes 409632 | tf_op jit(solution)/shard_map/ppermute | solution.py:31
  96.0 7.7 %collective-permute-done.9.refs_2_ = bf16[320,640]{1,0:T(8,128)(2,1)S(1)} collective-permute-done((bf16[320,640]{1,0:T(8,128)(2,1)S(1)}, bf16[320,640]{1,0:T(8,128)(2,1)S(1)}, u32[]{:S(2)}, u32[]{:S(2)}) %collective-permute-start.9) | collective-permute-done | bytes 409632 | tf_op jit(solution)/shard_map/ppermute | solution.py:32
  103.8 3.4 %collective-permute-start.3 = (bf16[320,640]{1,0:T(8,128)(2,1)S(1)}, bf16[320,640]{1,0:T(8,128)(2,1)S(1)}, u32[]{:S(2)}, u32[]{:S(2)}) collective-permute-start(bf16[320,640]{1,0:T(8,128)(2,1)S(1)} %collective-permute-done.2.refs_2_), channel_id=1, source_target_pairs={{0,7},{1,0},{2,1},{3,2},{4,3},{5,4},{6,5},{7,6},{8,15},{9,8},{10,9... | collective-permute-start | bytes 1228808 | tf_op jit(solution)/shard_map/ppermute | solution.py:32
  107.2 3.7 %collective-permute-done.21.refs_10_.mine_mid = bf16[328,896]{1,0:T(8,128)(2,1)S(1)} collective-permute-done((bf16[328,896]{1,0:T(8,128)(2,1)}, bf16[328,896]{1,0:T(8,128)(2,1)S(1)}, u32[]{:S(2)}, u32[]{:S(2)}) %collective-permute-start.21) | collective-permute-done | bytes 587808 | tf_op jit(solution)/shard_map/ppermute | solution.py:38
  111.0 2.2 %collective-permute-start.22 = (bf16[328,896]{1,0:T(8,128)(2,1)S(1)}, bf16[328,896]{1,0:T(8,128)(2,1)S(1)}, u32[]{:S(2)}, u32[]{:S(2)}) collective-permute-start(bf16[328,896]{1,0:T(8,128)(2,1)S(1)} %collective-permute-done.21.refs_10_.mine_mid), channel_id=1, source_target_pairs={{0,8},{8,0},{16,24},{24,16},{32,40},{40,32},{48,56},{56,48},{64,72... | collective-permute-start | bytes 1763336 | tf_op jit(solution)/shard_map/ppermute | solution.py:46
  113.6 1.3 collective-permute-done.3.refs_3_
  115.4 8.2 %collective-permute-done.10.refs_3_ = bf16[320,640]{1,0:T(8,128)(2,1)S(1)} collective-permute-done((bf16[320,640]{1,0:T(8,128)(2,1)S(1)}, bf16[320,640]{1,0:T(8,128)(2,1)S(1)}, u32[]{:S(2)}, u32[]{:S(2)}) %collective-permute-start.10) | collective-permute-done | bytes 409632 | tf_op jit(solution)/shard_map/ppermute | solution.py:32
  123.7 3.4 %collective-permute-start.11 = (bf16[320,640]{1,0:T(8,128)(2,1)S(1)}, bf16[320,640]{1,0:T(8,128)(2,1)S(1)}, u32[]{:S(2)}, u32[]{:S(2)}) collective-permute-start(bf16[320,640]{1,0:T(8,128)(2,1)S(1)} %collective-permute-done.10.refs_3_), channel_id=1, source_target_pairs={{0,7},{1,0},{2,1},{3,2},{4,3},{5,4},{6,5},{7,6},{8,15},{9,8},{10,9... | collective-permute-start | bytes 1228808 | tf_op jit(solution)/shard_map/ppermute | solution.py:40
  127.1 1.9 shard_map.95.x_a
  129.0 4.7 %collective-permute-done.13.refs_5_ = bf16[320,640]{1,0:T(8,128)(2,1)S(1)} collective-permute-done((bf16[320,640]{1,0:T(8,128)(2,1)S(1)}, bf16[320,640]{1,0:T(8,128)(2,1)S(1)}, u32[]{:S(2)}, u32[]{:S(2)}) %collective-permute-start.13) | collective-permute-done | bytes 409632 | tf_op jit(solution)/shard_map/ppermute | solution.py:31
  133.9 4.9 %shard_map.96 = (bf16[640,256]{1,0:T(8,128)(2,1)S(1)}, s32[16,128]{1,0:T(8,128)S(1)}, bf16[320,5120]{1,0:T(8,128)(2,1)S(1)}) custom-call(s32[4]{0:T(128)S(1)} %pad_add_fusion.place, bf16[320,5120]{1,0:T(8,128)(2,1)S(1)} %shard_map.95.x_a, bf16[320,640]{1,0:T(8,128)(2,1)S(1)} %get-tuple-element.21.refs_0_, ...), custom_call_target="tpu_custom_call" | custom-call | flops 1677721600 | bytes 13107200 | tf_op jit(solution)/shard_map/pallas_call | solution.py:177
  138.9 1.4 collective-permute-start.23
  140.4 5.0 %collective-permute-done.25 = bf16[640,256]{1,0:T(8,128)(2,1)S(1)} collective-permute-done((bf16[640,256]{1,0:T(8,128)(2,1)S(1)}, bf16[640,256]{1,0:T(8,128)(2,1)S(1)}, u32[]{:S(2)}, u32[]{:S(2)}) %collective-permute-start.25) | collective-permute-done | bytes 327712 | tf_op jit(solution)/shard_map/ppermute | solution.py:32
  145.3 1.5 collective-permute-start.26
  146.9 5.0 %collective-permute-done.26 = bf16[640,256]{1,0:T(8,128)(2,1)S(1)} collective-permute-done((bf16[640,256]{1,0:T(8,128)(2,1)S(1)}, bf16[640,256]{1,0:T(8,128)(2,1)S(1)}, u32[]{:S(2)}, u32[]{:S(2)}) %collective-permute-start.26) | collective-permute-done | bytes 327712 | tf_op jit(solution)/shard_map/ppermute | solution.py:32
  151.8 2.1 %collective-permute-start.28 = (bf16[640,256]{1,0:T(8,128)(2,1)S(1)}, bf16[640,256]{1,0:T(8,128)(2,1)S(1)}, u32[]{:S(2)}, u32[]{:S(2)}) collective-permute-start(bf16[640,256]{1,0:T(8,128)(2,1)S(1)} %collective-permute-done.26), channel_id=1, source_target_pairs={{0,112},{8,120},{16,0},{24,8},{32,16},{40,24},{48,32},{56,40},{64,... | collective-permute-start | bytes 983048 | tf_op jit(solution)/shard_map/ppermute | solution.py:32
  154.2 5.3 %collective-permute-done.28 = bf16[640,256]{1,0:T(8,128)(2,1)S(1)} collective-permute-done((bf16[640,256]{1,0:T(8,128)(2,1)S(1)}, bf16[640,256]{1,0:T(8,128)(2,1)S(1)}, u32[]{:S(2)}, u32[]{:S(2)}) %collective-permute-start.28) | collective-permute-done | bytes 327712 | tf_op jit(solution)/shard_map/ppermute | solution.py:32
  159.5 2.1 %collective-permute-done.29 = bf16[640,256]{1,0:T(8,128)(2,1)S(1)} collective-permute-done((bf16[640,256]{1,0:T(8,128)(2,1)S(1)}, bf16[640,256]{1,0:T(8,128)(2,1)S(1)}, u32[]{:S(2)}, u32[]{:S(2)}) %collective-permute-start.29) | collective-permute-done | bytes 327712 | tf_op jit(solution)/shard_map/ppermute | solution.py:31
  161.7 6.0 %collective-permute-start.30 = (bf16[4480,256]{1,0:T(8,128)(2,1)S(1)}, bf16[4480,256]{1,0:T(8,128)(2,1)S(1)}, u32[]{:S(2)}, u32[]{:S(2)}) collective-permute-start(bf16[4480,256]{1,0:T(8,128)(2,1)S(1)} %constant_dynamic-update-slice_fusion.mine), channel_id=1, source_target_pairs={{0,8},{8,0},{16,24},{24,16},{32,40},{40,32},{48,56},{56,48},{64,72... | collective-permute-start | bytes 6881288 | tf_op jit(solution)/shard_map/ppermute | solution.py:46
  167.7 1.9 collective-permute-start.24
  169.6 8.8 %shard_map.97.q_in = bf16[5,640,128]{2,1,0:T(8,128)(2,1)S(1)} custom-call(s32[4]{0:T(128)S(1)} %pad_add_fusion.place, bf16[320,5120]{1,0:T(8,128)(2,1)S(1)} %shard_map.95.x_a, bf16[320,5120]{1,0:T(8,128)(2,1)S(1)} %get-tuple-element.17.x_b, bf16[7,328,896]{2,1,0:T(8,128)(2,1)} %bitcast_dynamic-update-slice_fusion.refs_8_.mine, ...), custom_call_target="tpu_custom_call" | custom-call | flops 4194304000 | bytes 6553600 | tf_op jit(solution)/shard_map/pallas_call | solution.py:210
  178.6 6.1 %shard_map.98.refs_0_ = bf16[640,640]{1,0:T(8,128)(2,1)} custom-call(s32[9]{0:T(128)S(1)} %pad_add_fusion.1.info, bf16[5,640,128]{2,1,0:T(8,128)(2,1)S(1)} %shard_map.97.q_in, bf16[640,256]{1,0:T(8,128)(2,1)S(1)} %collective-permute-done.23.far, bf16[640,256]{1,0:T(8,128)(2,1)S(1)} %collective-permute-done.24.near, bf16[640,256]{1,0:T(8,128)(2,1)S(1)} %get-tuple-element.18.own), custom_call_target="tpu_custom_call" | custom-call | flops 4000000000 | bytes 4000000 | tf_op jit(solution)/shard_map/pallas_call | solution.py:340
  184.7 2.6 %collective-permute-done.31.mine_mid = bf16[640,256]{1,0:T(8,128)(2,1)S(1)} collective-permute-done((bf16[640,256]{1,0:T(8,128)(2,1)S(1)}, bf16[640,256]{1,0:T(8,128)(2,1)S(1)}, u32[]{:S(2)}, u32[]{:S(2)}) %collective-permute-start.31) | collective-permute-done | bytes 327712 | tf_op jit(solution)/shard_map/ppermute | solution.py:40
  187.3 1.4 collective-permute-start.32
  188.7 7.2 %shard_map.99.refs_0_ = bf16[640,640]{1,0:T(8,128)(2,1)} custom-call(s32[9]{0:T(128)S(1)} %pad_add_fusion.1.info, bf16[5,640,128]{2,1,0:T(8,128)(2,1)S(1)} %shard_map.97.q_in, bf16[640,256]{1,0:T(8,128)(2,1)S(1)} %collective-permute-done.23.far, bf16[640,256]{1,0:T(8,128)(2,1)S(1)} %collective-permute-done.24.near, ...), custom_call_target="tpu_custom_call", output_to_operand_aliasing={{}: (5, {})} | custom-call | flops 4000000000 | bytes 4000000 | tf_op jit(solution)/shard_map/pallas_call | solution.py:340
  195.9 2.5 %shard_map.100 = bf16[640,640]{1,0:T(8,128)(2,1)} custom-call(s32[9]{0:T(128)S(1)} %pad_add_fusion.1.info, bf16[5,640,128]{2,1,0:T(8,128)(2,1)S(1)} %shard_map.97.q_in, bf16[640,256]{1,0:T(8,128)(2,1)S(1)} %collective-permute-done.23.far, bf16[640,256]{1,0:T(8,128)(2,1)S(1)} %collective-permute-done.24.near, ...), custom_call_target="tpu_custom_call", output_to_operand_aliasing={{}: (5, {})} | custom-call | flops 2000000000 | bytes 4000000 | tf_op jit(solution)/shard_map/pallas_call | solution.py:340
  198.4 3.3 %shard_map.101 = bf16[32,128,256]{2,1,0:T(8,128)(2,1)} custom-call(s32[4]{0:T(128)S(1)} %pad_add_fusion.place, s32[16,128]{1,0:T(8,128)S(1)} %get-tuple-element.19.labels, s32[1,32]{1,0:T(1,128)S(1)} %copy-done, bf16[4480,256]{1,0:T(8,128)(2,1)S(1)} %constant_dynamic-update-slice_fusion.mine, bf16[4480,256]{1,0:T(8,128)(2,1)S(1)} %collective-permute-done.30.other, ...), custom_call_target="tpu_custom_call" | custom-call | tf_op jit(solution)/shard_map/pallas_call | solution.py:424
  (63 shorter events, 6.1 us)
Async XLA Ops:
  2.4 19.3 %collective-permute-start.14 = (bf16[328,896]{1,0:T(8,128)(2,1)S(1)}, bf16[328,896]{1,0:T(8,128)(2,1)S(1)}, u32[]{:S(2)}, u32[]{:S(2)}) collective-permute-start(bf16[328,896]{1,0:T(8,128)(2,1)S(1)} %fusion.1), channel_id=1, source_target_pairs={{0,112},{8,120},{16,0},{24,8},{32,16},{40,24},{48,32},{56,40},{64,... | collective-permute-start | bytes 1763336 | tf_op jit(solution)/shard_map/ppermute | solution.py:32
  15.0 12.2 %collective-permute-start.15 = (bf16[328,896]{1,0:T(8,128)(2,1)S(1)}, bf16[328,896]{1,0:T(8,128)(2,1)S(1)}, u32[]{:S(2)}, u32[]{:S(2)}) collective-permute-start(bf16[328,896]{1,0:T(8,128)(2,1)S(1)} %fusion.1), channel_id=1, source_target_pairs={{0,16},{8,24},{16,32},{24,40},{32,48},{40,56},{48,64},{56,72},{64,... | collective-permute-start | bytes 1763336 | tf_op jit(solution)/shard_map/ppermute | solution.py:31
  21.8 14.5 %collective-permute-start.16 = (bf16[328,896]{1,0:T(8,128)(2,1)S(1)}, bf16[328,896]{1,0:T(8,128)(2,1)S(1)}, u32[]{:S(2)}, u32[]{:S(2)}) collective-permute-start(bf16[328,896]{1,0:T(8,128)(2,1)S(1)} %collective-permute-done.14), channel_id=1, source_target_pairs={{0,112},{8,120},{16,0},{24,8},{32,16},{40,24},{48,32},{56,40},{64,... | collective-permute-start | bytes 1763336 | tf_op jit(solution)/shard_map/ppermute | solution.py:32
  27.2 13.1 %collective-permute-start.17 = (bf16[328,896]{1,0:T(8,128)(2,1)S(1)}, bf16[328,896]{1,0:T(8,128)(2,1)S(1)}, u32[]{:S(2)}, u32[]{:S(2)}) collective-permute-start(bf16[328,896]{1,0:T(8,128)(2,1)S(1)} %collective-permute-done.15), channel_id=1, source_target_pairs={{0,16},{8,24},{16,32},{24,40},{32,48},{40,56},{48,64},{56,72},{64,... | collective-permute-start | bytes 1763336 | tf_op jit(solution)/shard_map/ppermute | solution.py:31
  36.3 14.5 %collective-permute-start.18 = (bf16[328,896]{1,0:T(8,128)(2,1)S(1)}, bf16[328,896]{1,0:T(8,128)(2,1)S(1)}, u32[]{:S(2)}, u32[]{:S(2)}) collective-permute-start(bf16[328,896]{1,0:T(8,128)(2,1)S(1)} %collective-permute-done.16), channel_id=1, source_target_pairs={{0,112},{8,120},{16,0},{24,8},{32,16},{40,24},{48,32},{56,40},{64,... | collective-permute-start | bytes 1763336 | tf_op jit(solution)/shard_map/ppermute | solution.py:32
  40.2 25.8 %copy-start.1 = (bf16[640,640]{1,0:T(8,128)(2,1)S(1)}, bf16[640,640]{1,0:T(8,128)(2,1)}, u32[]{:S(2)}) copy-start(bf16[640,640]{1,0:T(8,128)(2,1)} %param.8) | copy-start | bytes 2457604
  40.3 13.9 %collective-permute-start.19 = (bf16[328,896]{1,0:T(8,128)(2,1)S(1)}, bf16[328,896]{1,0:T(8,128)(2,1)S(1)}, u32[]{:S(2)}, u32[]{:S(2)}) collective-permute-start(bf16[328,896]{1,0:T(8,128)(2,1)S(1)} %collective-permute-done.17), channel_id=1, source_target_pairs={{0,16},{8,24},{16,32},{24,40},{32,48},{40,56},{48,64},{56,72},{64,... | collective-permute-start | bytes 1763336 | tf_op jit(solution)/shard_map/ppermute | solution.py:31
  42.2 28.2 %copy-start.4 = (s32[8]{0:T(128)S(1)}, s32[8]{0:T(128)}, u32[]{:S(2)}) copy-start(s32[8]{0:T(128)} %param.13) | copy-start | bytes 100
  42.2 36.3 %copy-start.3 = (bf16[5120]{0:T(1024)(128)(2,1)S(1)}, bf16[5120]{0:T(1024)(128)(2,1)}, u32[]{:S(2)}) copy-start(bf16[5120]{0:T(1024)(128)(2,1)} %param.9) | copy-start | bytes 30724
  54.2 12.0 %copy-start.2 = (bf16[328,896]{1,0:T(8,128)(2,1)}, bf16[328,896]{1,0:T(8,128)(2,1)S(1)}, u32[]{:S(2)}) copy-start(bf16[328,896]{1,0:T(8,128)(2,1)S(1)} %collective-permute-done.19) | copy-start | bytes 1763332
  55.1 78.8 %collective-permute-start.20 = (bf16[7,328,896]{2,1,0:T(8,128)(2,1)}, bf16[7,328,896]{2,1,0:T(8,128)(2,1)}, u32[]{:S(2)}, u32[]{:S(2)}) collective-permute-start(bf16[7,328,896]{2,1,0:T(8,128)(2,1)} %bitcast_dynamic-update-slice_fusion.refs_8_.mine), channel_id=1, source_target_pairs={{0,8},{8,0},{16,24},{24,16},{32,40},{40,32},{48,56},{56,48},{64,72... | collective-permute-start | bytes 12343304 | tf_op jit(solution)/shard_map/ppermute | solution.py:46
  66.1 12.3 %collective-permute-start.4 = (bf16[320,640]{1,0:T(8,128)(2,1)S(1)}, bf16[320,640]{1,0:T(8,128)(2,1)S(1)}, u32[]{:S(2)}, u32[]{:S(2)}) collective-permute-start(bf16[320,640]{1,0:T(8,128)(2,1)S(1)} %get-tuple-element.20.refs_0_), channel_id=1, source_target_pairs={{0,1},{1,2},{2,3},{3,4},{4,5},{5,6},{6,7},{7,0},{8,9},{9,10},{10,1... | collective-permute-start | bytes 1228808 | tf_op jit(solution)/shard_map/ppermute | solution.py:31
  66.3 13.8 %collective-permute-start.1 = (bf16[320,640]{1,0:T(8,128)(2,1)S(1)}, bf16[320,640]{1,0:T(8,128)(2,1)S(1)}, u32[]{:S(2)}, u32[]{:S(2)}) collective-permute-start(bf16[320,640]{1,0:T(8,128)(2,1)S(1)} %get-tuple-element.20.refs_0_), channel_id=1, source_target_pairs={{0,7},{1,0},{2,1},{3,2},{4,3},{5,4},{6,5},{7,6},{8,15},{9,8},{10,9... | collective-permute-start | bytes 1228808 | tf_op jit(solution)/shard_map/ppermute | solution.py:32
  68.9 18.3 %collective-permute-start.8 = (bf16[320,640]{1,0:T(8,128)(2,1)S(1)}, bf16[320,640]{1,0:T(8,128)(2,1)S(1)}, u32[]{:S(2)}, u32[]{:S(2)}) collective-permute-start(bf16[320,640]{1,0:T(8,128)(2,1)S(1)} %get-tuple-element.21.refs_0_), channel_id=1, source_target_pairs={{0,7},{1,0},{2,1},{3,2},{4,3},{5,4},{6,5},{7,6},{8,15},{9,8},{10,9... | collective-permute-start | bytes 1228808 | tf_op jit(solution)/shard_map/ppermute | solution.py:32
  69.0 18.3 %collective-permute-start = (bf16[320,640]{1,0:T(8,128)(2,1)S(1)}, bf16[320,640]{1,0:T(8,128)(2,1)S(1)}, u32[]{:S(2)}, u32[]{:S(2)}) collective-permute-start(bf16[320,640]{1,0:T(8,128)(2,1)S(1)} %get-tuple-element.21.refs_0_), channel_id=1, source_target_pairs={{0,1},{1,2},{2,3},{3,4},{4,5},{5,6},{6,7},{7,0},{8,9},{9,10},{10,1... | collective-permute-start | bytes 1228808 | tf_op jit(solution)/shard_map/ppermute | solution.py:31
  78.5 17.6 %collective-permute-start.5 = (bf16[320,640]{1,0:T(8,128)(2,1)S(1)}, bf16[320,640]{1,0:T(8,128)(2,1)S(1)}, u32[]{:S(2)}, u32[]{:S(2)}) collective-permute-start(bf16[320,640]{1,0:T(8,128)(2,1)S(1)} %collective-permute-done.4.refs_7_), channel_id=1, source_target_pairs={{0,1},{1,2},{2,3},{3,4},{4,5},{5,6},{6,7},{7,0},{8,9},{9,10},{10,1... | collective-permute-start | bytes 1228808 | tf_op jit(solution)/shard_map/ppermute | solution.py:31
  80.1 16.0 %collective-permute-start.2 = (bf16[320,640]{1,0:T(8,128)(2,1)S(1)}, bf16[320,640]{1,0:T(8,128)(2,1)S(1)}, u32[]{:S(2)}, u32[]{:S(2)}) collective-permute-start(bf16[320,640]{1,0:T(8,128)(2,1)S(1)} %collective-permute-done.1.refs_1_), channel_id=1, source_target_pairs={{0,7},{1,0},{2,1},{3,2},{4,3},{5,4},{6,5},{7,6},{8,15},{9,8},{10,9... | collective-permute-start | bytes 1228808 | tf_op jit(solution)/shard_map/ppermute | solution.py:32
  87.2 16.5 %collective-permute-start.9 = (bf16[320,640]{1,0:T(8,128)(2,1)S(1)}, bf16[320,640]{1,0:T(8,128)(2,1)S(1)}, u32[]{:S(2)}, u32[]{:S(2)}) collective-permute-start(bf16[320,640]{1,0:T(8,128)(2,1)S(1)} %collective-permute-done.8.refs_1_), channel_id=1, source_target_pairs={{0,7},{1,0},{2,1},{3,2},{4,3},{5,4},{6,5},{7,6},{8,15},{9,8},{10,9... | collective-permute-start | bytes 1228808 | tf_op jit(solution)/shard_map/ppermute | solution.py:32
  89.6 17.6 %collective-permute-start.12 = (bf16[320,640]{1,0:T(8,128)(2,1)S(1)}, bf16[320,640]{1,0:T(8,128)(2,1)S(1)}, u32[]{:S(2)}, u32[]{:S(2)}) collective-permute-start(bf16[320,640]{1,0:T(8,128)(2,1)S(1)} %collective-permute-done.refs_7_), channel_id=1, source_target_pairs={{0,1},{1,2},{2,3},{3,4},{4,5},{5,6},{6,7},{7,0},{8,9},{9,10},{10,1... | collective-permute-start | bytes 1228808 | tf_op jit(solution)/shard_map/ppermute | solution.py:31
  96.0 14.9 %collective-permute-start.21 = (bf16[328,896]{1,0:T(8,128)(2,1)}, bf16[328,896]{1,0:T(8,128)(2,1)S(1)}, u32[]{:S(2)}, u32[]{:S(2)}) collective-permute-start(bf16[328,896]{1,0:T(8,128)(2,1)} %copy-done.2), channel_id=1, source_target_pairs={{0,16},{8,24},{16,32},{24,40},{32,48},{40,56},{48,64},{56,72},{64,... | collective-permute-start | bytes 1763336 | tf_op jit(solution)/shard_map/ppermute | solution.py:38
  96.0 17.5 %collective-permute-start.6 = (bf16[320,640]{1,0:T(8,128)(2,1)S(1)}, bf16[320,640]{1,0:T(8,128)(2,1)S(1)}, u32[]{:S(2)}, u32[]{:S(2)}) collective-permute-start(bf16[320,640]{1,0:T(8,128)(2,1)S(1)} %collective-permute-done.5.refs_6_), channel_id=1, source_target_pairs={{0,1},{1,2},{2,3},{3,4},{4,5},{5,6},{6,7},{7,0},{8,9},{9,10},{10,1... | collective-permute-start | bytes 1228808 | tf_op jit(solution)/shard_map/ppermute | solution.py:31
  103.8 11.1 %collective-permute-start.3 = (bf16[320,640]{1,0:T(8,128)(2,1)S(1)}, bf16[320,640]{1,0:T(8,128)(2,1)S(1)}, u32[]{:S(2)}, u32[]{:S(2)}) collective-permute-start(bf16[320,640]{1,0:T(8,128)(2,1)S(1)} %collective-permute-done.2.refs_2_), channel_id=1, source_target_pairs={{0,7},{1,0},{2,1},{3,2},{4,3},{5,4},{6,5},{7,6},{8,15},{9,8},{10,9... | collective-permute-start | bytes 1228808 | tf_op jit(solution)/shard_map/ppermute | solution.py:32
  107.2 16.5 %collective-permute-start.10 = (bf16[320,640]{1,0:T(8,128)(2,1)S(1)}, bf16[320,640]{1,0:T(8,128)(2,1)S(1)}, u32[]{:S(2)}, u32[]{:S(2)}) collective-permute-start(bf16[320,640]{1,0:T(8,128)(2,1)S(1)} %collective-permute-done.9.refs_2_), channel_id=1, source_target_pairs={{0,7},{1,0},{2,1},{3,2},{4,3},{5,4},{6,5},{7,6},{8,15},{9,8},{10,9... | collective-permute-start | bytes 1228808 | tf_op jit(solution)/shard_map/ppermute | solution.py:32
  111.0 22.9 %collective-permute-start.22 = (bf16[328,896]{1,0:T(8,128)(2,1)S(1)}, bf16[328,896]{1,0:T(8,128)(2,1)S(1)}, u32[]{:S(2)}, u32[]{:S(2)}) collective-permute-start(bf16[328,896]{1,0:T(8,128)(2,1)S(1)} %collective-permute-done.21.refs_10_.mine_mid), channel_id=1, source_target_pairs={{0,8},{8,0},{16,24},{24,16},{32,40},{40,32},{48,56},{56,48},{64,72... | collective-permute-start | bytes 1763336 | tf_op jit(solution)/shard_map/ppermute | solution.py:46
  113.6 13.5 %collective-permute-start.7 = (bf16[320,640]{1,0:T(8,128)(2,1)S(1)}, bf16[320,640]{1,0:T(8,128)(2,1)S(1)}, u32[]{:S(2)}, u32[]{:S(2)}) collective-permute-start(bf16[320,640]{1,0:T(8,128)(2,1)S(1)} %collective-permute-done.6.refs_5_), channel_id=1, source_target_pairs={{0,1},{1,2},{2,3},{3,4},{4,5},{5,6},{6,7},{7,0},{8,9},{9,10},{10,1... | collective-permute-start | bytes 1228808 | tf_op jit(solution)/shard_map/ppermute | solution.py:38
  114.9 18.8 %collective-permute-start.13 = (bf16[320,640]{1,0:T(8,128)(2,1)S(1)}, bf16[320,640]{1,0:T(8,128)(2,1)S(1)}, u32[]{:S(2)}, u32[]{:S(2)}) collective-permute-start(bf16[320,640]{1,0:T(8,128)(2,1)S(1)} %collective-permute-done.12.refs_6_), channel_id=1, source_target_pairs={{0,1},{1,2},{2,3},{3,4},{4,5},{5,6},{6,7},{7,0},{8,9},{9,10},{10,1... | collective-permute-start | bytes 1228808 | tf_op jit(solution)/shard_map/ppermute | solution.py:31
  123.7 10.2 %collective-permute-start.11 = (bf16[320,640]{1,0:T(8,128)(2,1)S(1)}, bf16[320,640]{1,0:T(8,128)(2,1)S(1)}, u32[]{:S(2)}, u32[]{:S(2)}) collective-permute-start(bf16[320,640]{1,0:T(8,128)(2,1)S(1)} %collective-permute-done.10.refs_3_), channel_id=1, source_target_pairs={{0,7},{1,0},{2,1},{3,2},{4,3},{5,4},{6,5},{7,6},{8,15},{9,8},{10,9... | collective-permute-start | bytes 1228808 | tf_op jit(solution)/shard_map/ppermute | solution.py:40
  138.8 6.5 %collective-permute-start.25 = (bf16[640,256]{1,0:T(8,128)(2,1)S(1)}, bf16[640,256]{1,0:T(8,128)(2,1)S(1)}, u32[]{:S(2)}, u32[]{:S(2)}) collective-permute-start(bf16[640,256]{1,0:T(8,128)(2,1)S(1)} %get-tuple-element.18.own), channel_id=1, source_target_pairs={{0,112},{8,120},{16,0},{24,8},{32,16},{40,24},{48,32},{56,40},{64,... | collective-permute-start | bytes 983048 | tf_op jit(solution)/shard_map/ppermute | solution.py:32
  138.9 7.9 %collective-permute-start.23 = (bf16[640,256]{1,0:T(8,128)(2,1)S(1)}, bf16[640,256]{1,0:T(8,128)(2,1)S(1)}, u32[]{:S(2)}, u32[]{:S(2)}) collective-permute-start(bf16[640,256]{1,0:T(8,128)(2,1)S(1)} %get-tuple-element.18.own), channel_id=1, source_target_pairs={{0,16},{8,24},{16,32},{24,40},{32,48},{40,56},{48,64},{56,72},{64,... | collective-permute-start | bytes 983048 | tf_op jit(solution)/shard_map/ppermute | solution.py:31
  145.3 6.5 %collective-permute-start.26 = (bf16[640,256]{1,0:T(8,128)(2,1)S(1)}, bf16[640,256]{1,0:T(8,128)(2,1)S(1)}, u32[]{:S(2)}, u32[]{:S(2)}) collective-permute-start(bf16[640,256]{1,0:T(8,128)(2,1)S(1)} %collective-permute-done.25), channel_id=1, source_target_pairs={{0,112},{8,120},{16,0},{24,8},{32,16},{40,24},{48,32},{56,40},{64,... | collective-permute-start | bytes 983048 | tf_op jit(solution)/shard_map/ppermute | solution.py:32
  146.8 7.2 %collective-permute-start.27 = (bf16[640,256]{1,0:T(8,128)(2,1)S(1)}, bf16[640,256]{1,0:T(8,128)(2,1)S(1)}, u32[]{:S(2)}, u32[]{:S(2)}) collective-permute-start(bf16[640,256]{1,0:T(8,128)(2,1)S(1)} %collective-permute-done.23.far), channel_id=1, source_target_pairs={{0,16},{8,24},{16,32},{24,40},{32,48},{40,56},{48,64},{56,72},{64,... | collective-permute-start | bytes 983048 | tf_op jit(solution)/shard_map/ppermute | solution.py:31
  151.8 7.7 %collective-permute-start.28 = (bf16[640,256]{1,0:T(8,128)(2,1)S(1)}, bf16[640,256]{1,0:T(8,128)(2,1)S(1)}, u32[]{:S(2)}, u32[]{:S(2)}) collective-permute-start(bf16[640,256]{1,0:T(8,128)(2,1)S(1)} %collective-permute-done.26), channel_id=1, source_target_pairs={{0,112},{8,120},{16,0},{24,8},{32,16},{40,24},{48,32},{56,40},{64,... | collective-permute-start | bytes 983048 | tf_op jit(solution)/shard_map/ppermute | solution.py:32
  154.0 7.6 %collective-permute-start.29 = (bf16[640,256]{1,0:T(8,128)(2,1)S(1)}, bf16[640,256]{1,0:T(8,128)(2,1)S(1)}, u32[]{:S(2)}, u32[]{:S(2)}) collective-permute-start(bf16[640,256]{1,0:T(8,128)(2,1)S(1)} %collective-permute-done.27), channel_id=1, source_target_pairs={{0,16},{8,24},{16,32},{24,40},{32,48},{40,56},{48,64},{56,72},{64,... | collective-permute-start | bytes 983048 | tf_op jit(solution)/shard_map/ppermute | solution.py:31
  161.7 36.7 %collective-permute-start.30 = (bf16[4480,256]{1,0:T(8,128)(2,1)S(1)}, bf16[4480,256]{1,0:T(8,128)(2,1)S(1)}, u32[]{:S(2)}, u32[]{:S(2)}) collective-permute-start(bf16[4480,256]{1,0:T(8,128)(2,1)S(1)} %constant_dynamic-update-slice_fusion.mine), channel_id=1, source_target_pairs={{0,8},{8,0},{16,24},{24,16},{32,40},{40,32},{48,56},{56,48},{64,72... | collective-permute-start | bytes 6881288 | tf_op jit(solution)/shard_map/ppermute | solution.py:46
  167.7 10.9 %collective-permute-start.24 = (bf16[640,256]{1,0:T(8,128)(2,1)S(1)}, bf16[640,256]{1,0:T(8,128)(2,1)S(1)}, u32[]{:S(2)}, u32[]{:S(2)}) collective-permute-start(bf16[640,256]{1,0:T(8,128)(2,1)S(1)} %get-tuple-element.18.own), channel_id=1, source_target_pairs={{0,8},{8,16},{16,24},{24,32},{32,40},{40,48},{48,56},{56,64},{64,7... | collective-permute-start | bytes 983048 | tf_op jit(solution)/shard_map/ppermute | solution.py:485
  178.4 8.9 %collective-permute-start.31 = (bf16[640,256]{1,0:T(8,128)(2,1)S(1)}, bf16[640,256]{1,0:T(8,128)(2,1)S(1)}, u32[]{:S(2)}, u32[]{:S(2)}) collective-permute-start(bf16[640,256]{1,0:T(8,128)(2,1)S(1)} %collective-permute-done.28), channel_id=1, source_target_pairs={{0,112},{8,120},{16,0},{24,8},{32,16},{40,24},{48,32},{56,40},{64,... | collective-permute-start | bytes 983048 | tf_op jit(solution)/shard_map/ppermute | solution.py:40
  187.3 11.1 %collective-permute-start.32 = (bf16[640,256]{1,0:T(8,128)(2,1)S(1)}, bf16[640,256]{1,0:T(8,128)(2,1)S(1)}, u32[]{:S(2)}, u32[]{:S(2)}) collective-permute-start(bf16[640,256]{1,0:T(8,128)(2,1)S(1)} %collective-permute-done.31.mine_mid), channel_id=1, source_target_pairs={{0,8},{8,0},{16,24},{24,16},{32,40},{40,32},{48,56},{56,48},{64,72... | collective-permute-start | bytes 983048 | tf_op jit(solution)/shard_map/ppermute | solution.py:46
  195.9 2.6 %copy-start = (s32[1,32]{1,0:T(1,128)S(1)}, s32[1,32]{1,0:T(1,128)}, u32[]{:S(2)}) copy-start(s32[1,32]{1,0:T(1,128)} %table.1) | copy-start | bytes 388
